TPU v7x, 256 devices: a whole 4x4x8 slice. The times are simulated.
256 devices in a mesh: elem: 32 (over y_lo, z, core), test: 8 (over y_hi, x).
Axes of the slice: x: 4, y: 4 (y_hi: 2, y_lo: 2; y = y_hi * 2 + y_lo), z: 8, core: 2. Of those that a mesh axis runs over, the one named last changes fastest.
Arguments:
- mode_fields: bfloat16 [64, 3, 131072], P('test', None, 'elem'), may hold values from -6 to 6
- elem_type: int32 [256], P('elem'), may hold values from 0 to 3
- type_scales: float32 [4, 3], replicated, may hold values from 0.5 to 2
Outputs:
- conv_tensor: float32 [64, 64, 64], P('test', 'elem')
All inputs are finite; a program needn't handle non-finite values.
Results may differ from a plain program's by a relative error of at most 0.0051.
Values may be sent and summed in bfloat16 or wider, within the bound.
No kernel may reach another device: no remote copies, remote signals or barrier semaphores. Data moves between devices by JAX's collectives and lax.ppermute only.
A program may use at most 64 MiB of HBM per device.

v0:
```python
import jax
import jax.numpy as jnp
import numpy as np
from jax import lax
from jax.sharding import PartitionSpec as P

Q = 8


block_modes = 4


def laid_out(pieces, dim):
    pieces = jnp.moveaxis(pieces, 0, dim)
    lengths = pieces.shape
    return pieces.reshape(*lengths[:dim], lengths[dim] * lengths[dim + 1], *lengths[dim + 2 :])


def copy_for_each(array, axis):
    peers = lax.axis_size(axis)
    return lax.all_to_all(
        jnp.broadcast_to(array[None], (peers, *array.shape)), axis, 0, 0, tiled=True
    )


def gathered_copies(array, axis, dim):
    return laid_out(copy_for_each(array, axis), dim)


def in_blocks(array, dim, peers):
    lengths = array.shape
    pieces = array.reshape(*lengths[:dim], peers, lengths[dim] // peers, *lengths[dim + 1 :])
    return jnp.moveaxis(pieces, dim, 0)


def sum_at_owner(array, axis, dim):
    peers = lax.axis_size(axis)
    pieces = lax.all_to_all(in_blocks(array, dim, peers), axis, 0, 0, tiled=True)
    return jnp.sum(pieces, axis=0)


def legendre_top(points, degree):
    before = points * 0.0 + 1.0
    current = points
    for order in range(2, degree + 1):
        following = ((2 * order - 1) * points * current - (order - 1) * before) / order
        before = current
        current = following
    return (current, before)


def lobatto_tables(order_points):
    degree = order_points - 1
    lobatto_nodes = np.cos(np.pi * np.arange(degree + 1) / degree)
    for sweep in range(100):
        top, lower = legendre_top(lobatto_nodes, degree)
        lobatto_nodes = lobatto_nodes - (lobatto_nodes * top - lower) / ((degree + 1) * top)
    lobatto_nodes = lobatto_nodes[::-1].copy()
    lobatto_nodes[0] = -1.0
    lobatto_nodes[-1] = 1.0
    values, unused = legendre_top(lobatto_nodes, degree)
    weights = 2.0 / (degree * (degree + 1) * values**2)
    identity = np.eye(order_points)
    distance = lobatto_nodes[:, None] - lobatto_nodes[None, :]
    spacing = np.where(identity > 0, 1.0, distance)
    derivative = np.where(identity > 0, 0.0, values[:, None] / values[None, :] / spacing)
    corner = degree * (degree + 1) / 4.0
    ends = np.concatenate([[-corner], np.zeros(degree - 1), [corner]])
    derivative = derivative + identity * ends[None, :]
    square_eye = np.eye(order_points * order_points)
    along_r = np.kron(square_eye, derivative)
    along_s = np.kron(identity, np.kron(derivative, identity))
    along_t = np.kron(derivative, square_eye)
    table = np.concatenate([along_r.T, along_s.T, along_t.T], axis=1)
    cube_weights = np.kron(weights, np.kron(weights, weights))
    return (table.astype(np.float32), cube_weights.astype(np.float32))


def element_scales(types, type_scales):
    picks = (types[:, None] == jnp.arange(type_scales.shape[0], dtype=jnp.int32)[None, :]).astype(
        jnp.float32
    )
    return jnp.sum(picks[:, :, None] * type_scales[None, :, :], axis=1)


def gradient(fields, scales, table, cube):
    mode_count = fields.shape[0]
    elements = fields.shape[2] // cube
    flat = fields.reshape(mode_count * 3 * elements, cube)
    derived = jnp.dot(flat, table, preferred_element_type=jnp.float32).reshape(
        mode_count, 3, elements, 3, cube
    )
    return (derived * scales[None, None, :, :, None]).astype(jnp.bfloat16)


def project(test_fields, trial_fields, grads, quadrature):
    test_modes = test_fields.shape[0]
    trial_modes = trial_fields.shape[0]
    grad_modes = grads.shape[0]
    blocks = grads.reshape((grad_modes // block_modes, block_modes) + grads.shape[1:])
    test_wide = test_fields.astype(jnp.float32)

    def one_block(grad_block):
        grad_wide = grad_block.astype(jnp.float32)
        summed = test_wide[:, None, 0, :, None, :] * grad_wide[None, :, 0]
        summed = summed + test_wide[:, None, 1, :, None, :] * grad_wide[None, :, 1]
        summed = summed + test_wide[:, None, 2, :, None, :] * grad_wide[None, :, 2]
        pairs = (summed * quadrature[None, None, :, None, :]).astype(jnp.bfloat16)
        return jnp.einsum(
            "ikedp,jdep->ijk", pairs, trial_fields, preferred_element_type=jnp.float32
        )

    result = lax.map(one_block, blocks)
    return result.transpose(1, 2, 0, 3).reshape(test_modes, trial_modes, grad_modes)


def body(mode_fields, elem_type, type_scales):
    table, cube_weights = lobatto_tables(Q)
    table = jnp.asarray(table).astype(jnp.bfloat16)
    point_weights = jnp.asarray(cube_weights).astype(jnp.float32)
    cube = Q**3
    total_points = mode_fields.shape[2] * lax.axis_size("elem")
    gathered = gathered_copies(mode_fields, "test", 0)
    elements = mode_fields.shape[2] // cube
    scales = element_scales(elem_type, type_scales)
    quadrature = point_weights[None, :] / jnp.prod(scales, axis=1)[:, None]
    grads = gradient(gathered, scales, table, cube)
    partial_value = project(
        mode_fields.reshape(mode_fields.shape[0], 3, elements, cube),
        gathered.reshape(gathered.shape[0], 3, elements, cube),
        grads,
        quadrature,
    )
    summed = sum_at_owner(partial_value, "elem", 1)
    return summed * float(total_points) ** (-0.5)


def solution(mesh):
    placed = (P("test", None, "elem"), P("elem"), P())
    return jax.shard_map(
        body, mesh=mesh, in_specs=placed, out_specs=P("test", "elem", None), check_vma=False
    )
```

profile of v0, /device:TPU:8, one launch (start us, length us, event | category | flops | bytes accessed | tf_op | source)
XLA Modules:
  0.0 99.7 jit_solution(16699278084769694988)
XLA Ops:
  0.0 2.2 %broadcast_in_dim.8 = bf16[8,8,3,4096]{3,1,2,0:T(8,128)(2,1)} broadcast(bf16[8,3,4096]{2,0,1:T(8,128)(2,1)} %param.7), dimensions={1,2,3} | broadcast | bytes 1769472 | tf_op jit(solution)/shard_map/broadcast_in_dim | solution.py:22
  2.3 6.2 %all-to-all-start = ((bf16[8,8,3,4096]{3,1,2,0:T(8,128)(2,1)}), bf16[8,8,3,4096]{3,1,2,0:T(8,128)(2,1)S(1)}, u32[]{:S(2)}, u32[]{:S(2)}) async-start(bf16[8,8,3,4096]{3,1,2,0:T(8,128)(2,1)} %broadcast_in_dim.8), calls=%async_computation | async-start | bytes 3145728 | tf_op jit(solution)/shard_map/all_to_all | solution.py:21
  8.7 22.5 %all-to-all-done = bf16[8,8,3,4096]{3,1,2,0:T(8,128)(2,1)S(1)} async-done(((bf16[8,8,3,4096]{3,1,2,0:T(8,128)(2,1)}), bf16[8,8,3,4096]{3,1,2,0:T(8,128)(2,1)S(1)}, u32[]{:S(2)}, u32[]{:S(2)}) %all-to-all-start) | async-done | bytes 1572896 | tf_op jit(solution)/shard_map/all_to_all | solution.py:21
  33.5 4.3 %fusion.18 = bf16[64,3,8,3,512]{4,0,2,1,3:T(8,128)(2,1)} fusion(f32[8,3]{0,1:T(4,128)S(1)} %multiply_reduce_fusion, bf16[3,512,512,1,1]{2,1,4,3,0:T(8,128)(2,1)S(1)} %copy-done.4, bf16[64,3,8,512]{3,2,0,1:T(8,128)(2,1)S(1)} %bitcast.79), kind=kOutput, calls=%fused_computation.24 | convolution fusion | flops 2420637696 | bytes 7864416 | tf_op jit(solution)/shard_map/dot_general | solution.py:90
  37.8 7.7 %reshape.46 = bf16[16,4,3,8,3,512]{5,1,0,3,2,4:T(4,128)(2,1)} reshape(bf16[64,3,8,3,512]{4,0,2,1,3:T(8,128)(2,1)} %fusion.18) | data formatting | bytes 9437184 | tf_op jit(solution)/shard_map/reshape | solution.py:100
  45.5 29.9 %while.11 = (s32[]{:T(128)}, f32[16,8,64,4]{2,1,3,0:T(8,128)S(1)}, f32[8,3,8,512]{3,0,2,1:T(8,128)S(1)}, bf16[16,4,3,8,3,512]{5,1,0,3,2,4:T(4,128)(2,1)}, bf16[6...) while((s32[]{:T(128)}, f32[16,8,64,4]{2,1,3,0:T(8,128)S(1)}, ...), condition=%wide.region_3.4_spmd.clone, body=%wide.region_2.3_spmd.clone.sunk | while | flops 53235712 | bytes 6047869 | solution.py:113
  45.5 1.1 %constant_dynamic-slice_fusion.2 = bf16[1,4,3,8,3,512]{5,1,0,3,2,4:T(4,128)(2,1)S(1)} fusion(bf16[16,4,3,8,3,512]{5,1,0,3,2,4:T(4,128)(2,1)} %get-tuple-element.185, s32[]{:T(128)} %get-tuple-element.174), kind=kLoop, calls=%fused_computation.22.clone.1 | loop fusion | bytes 589828 | tf_op jit(solution)/shard_map/while/body/jit(dynamic_index_in_dim)/dynamic_slice | solution.py:113
  47.4 1.1 %constant_dynamic-slice_fusion.2 = bf16[1,4,3,8,3,512]{5,1,0,3,2,4:T(4,128)(2,1)S(1)} fusion(bf16[16,4,3,8,3,512]{5,1,0,3,2,4:T(4,128)(2,1)} %get-tuple-element.185, s32[]{:T(128)} %get-tuple-element.174), kind=kLoop, calls=%fused_computation.22.clone.1 | loop fusion | bytes 589828 | tf_op jit(solution)/shard_map/while/body/jit(dynamic_index_in_dim)/dynamic_slice | solution.py:113
  49.2 1.1 %constant_dynamic-slice_fusion.2 = bf16[1,4,3,8,3,512]{5,1,0,3,2,4:T(4,128)(2,1)S(1)} fusion(bf16[16,4,3,8,3,512]{5,1,0,3,2,4:T(4,128)(2,1)} %get-tuple-element.185, s32[]{:T(128)} %get-tuple-element.174), kind=kLoop, calls=%fused_computation.22.clone.1 | loop fusion | bytes 589828 | tf_op jit(solution)/shard_map/while/body/jit(dynamic_index_in_dim)/dynamic_slice | solution.py:113
  51.1 1.1 %constant_dynamic-slice_fusion.2 = bf16[1,4,3,8,3,512]{5,1,0,3,2,4:T(4,128)(2,1)S(1)} fusion(bf16[16,4,3,8,3,512]{5,1,0,3,2,4:T(4,128)(2,1)} %get-tuple-element.185, s32[]{:T(128)} %get-tuple-element.174), kind=kLoop, calls=%fused_computation.22.clone.1 | loop fusion | bytes 589828 | tf_op jit(solution)/shard_map/while/body/jit(dynamic_index_in_dim)/dynamic_slice | solution.py:113
  53.0 1.1 %constant_dynamic-slice_fusion.2 = bf16[1,4,3,8,3,512]{5,1,0,3,2,4:T(4,128)(2,1)S(1)} fusion(bf16[16,4,3,8,3,512]{5,1,0,3,2,4:T(4,128)(2,1)} %get-tuple-element.185, s32[]{:T(128)} %get-tuple-element.174), kind=kLoop, calls=%fused_computation.22.clone.1 | loop fusion | bytes 589828 | tf_op jit(solution)/shard_map/while/body/jit(dynamic_index_in_dim)/dynamic_slice | solution.py:113
  54.8 1.1 %constant_dynamic-slice_fusion.2 = bf16[1,4,3,8,3,512]{5,1,0,3,2,4:T(4,128)(2,1)S(1)} fusion(bf16[16,4,3,8,3,512]{5,1,0,3,2,4:T(4,128)(2,1)} %get-tuple-element.185, s32[]{:T(128)} %get-tuple-element.174), kind=kLoop, calls=%fused_computation.22.clone.1 | loop fusion | bytes 589828 | tf_op jit(solution)/shard_map/while/body/jit(dynamic_index_in_dim)/dynamic_slice | solution.py:113
  56.7 1.1 %constant_dynamic-slice_fusion.2 = bf16[1,4,3,8,3,512]{5,1,0,3,2,4:T(4,128)(2,1)S(1)} fusion(bf16[16,4,3,8,3,512]{5,1,0,3,2,4:T(4,128)(2,1)} %get-tuple-element.185, s32[]{:T(128)} %get-tuple-element.174), kind=kLoop, calls=%fused_computation.22.clone.1 | loop fusion | bytes 589828 | tf_op jit(solution)/shard_map/while/body/jit(dynamic_index_in_dim)/dynamic_slice | solution.py:113
  58.6 1.1 %constant_dynamic-slice_fusion.2 = bf16[1,4,3,8,3,512]{5,1,0,3,2,4:T(4,128)(2,1)S(1)} fusion(bf16[16,4,3,8,3,512]{5,1,0,3,2,4:T(4,128)(2,1)} %get-tuple-element.185, s32[]{:T(128)} %get-tuple-element.174), kind=kLoop, calls=%fused_computation.22.clone.1 | loop fusion | bytes 589828 | tf_op jit(solution)/shard_map/while/body/jit(dynamic_index_in_dim)/dynamic_slice | solution.py:113
  60.4 1.1 %constant_dynamic-slice_fusion.2 = bf16[1,4,3,8,3,512]{5,1,0,3,2,4:T(4,128)(2,1)S(1)} fusion(bf16[16,4,3,8,3,512]{5,1,0,3,2,4:T(4,128)(2,1)} %get-tuple-element.185, s32[]{:T(128)} %get-tuple-element.174), kind=kLoop, calls=%fused_computation.22.clone.1 | loop fusion | bytes 589828 | tf_op jit(solution)/shard_map/while/body/jit(dynamic_index_in_dim)/dynamic_slice | solution.py:113
  62.3 1.1 %constant_dynamic-slice_fusion.2 = bf16[1,4,3,8,3,512]{5,1,0,3,2,4:T(4,128)(2,1)S(1)} fusion(bf16[16,4,3,8,3,512]{5,1,0,3,2,4:T(4,128)(2,1)} %get-tuple-element.185, s32[]{:T(128)} %get-tuple-element.174), kind=kLoop, calls=%fused_computation.22.clone.1 | loop fusion | bytes 589828 | tf_op jit(solution)/shard_map/while/body/jit(dynamic_index_in_dim)/dynamic_slice | solution.py:113
  64.2 1.1 %constant_dynamic-slice_fusion.2 = bf16[1,4,3,8,3,512]{5,1,0,3,2,4:T(4,128)(2,1)S(1)} fusion(bf16[16,4,3,8,3,512]{5,1,0,3,2,4:T(4,128)(2,1)} %get-tuple-element.185, s32[]{:T(128)} %get-tuple-element.174), kind=kLoop, calls=%fused_computation.22.clone.1 | loop fusion | bytes 589828 | tf_op jit(solution)/shard_map/while/body/jit(dynamic_index_in_dim)/dynamic_slice | solution.py:113
  66.0 1.1 %constant_dynamic-slice_fusion.2 = bf16[1,4,3,8,3,512]{5,1,0,3,2,4:T(4,128)(2,1)S(1)} fusion(bf16[16,4,3,8,3,512]{5,1,0,3,2,4:T(4,128)(2,1)} %get-tuple-element.185, s32[]{:T(128)} %get-tuple-element.174), kind=kLoop, calls=%fused_computation.22.clone.1 | loop fusion | bytes 589828 | tf_op jit(solution)/shard_map/while/body/jit(dynamic_index_in_dim)/dynamic_slice | solution.py:113
  67.9 1.1 %constant_dynamic-slice_fusion.2 = bf16[1,4,3,8,3,512]{5,1,0,3,2,4:T(4,128)(2,1)S(1)} fusion(bf16[16,4,3,8,3,512]{5,1,0,3,2,4:T(4,128)(2,1)} %get-tuple-element.185, s32[]{:T(128)} %get-tuple-element.174), kind=kLoop, calls=%fused_computation.22.clone.1 | loop fusion | bytes 589828 | tf_op jit(solution)/shard_map/while/body/jit(dynamic_index_in_dim)/dynamic_slice | solution.py:113
  69.8 1.1 %constant_dynamic-slice_fusion.2 = bf16[1,4,3,8,3,512]{5,1,0,3,2,4:T(4,128)(2,1)S(1)} fusion(bf16[16,4,3,8,3,512]{5,1,0,3,2,4:T(4,128)(2,1)} %get-tuple-element.185, s32[]{:T(128)} %get-tuple-element.174), kind=kLoop, calls=%fused_computation.22.clone.1 | loop fusion | bytes 589828 | tf_op jit(solution)/shard_map/while/body/jit(dynamic_index_in_dim)/dynamic_slice | solution.py:113
  71.6 1.1 %constant_dynamic-slice_fusion.2 = bf16[1,4,3,8,3,512]{5,1,0,3,2,4:T(4,128)(2,1)S(1)} fusion(bf16[16,4,3,8,3,512]{5,1,0,3,2,4:T(4,128)(2,1)} %get-tuple-element.185, s32[]{:T(128)} %get-tuple-element.174), kind=kLoop, calls=%fused_computation.22.clone.1 | loop fusion | bytes 589828 | tf_op jit(solution)/shard_map/while/body/jit(dynamic_index_in_dim)/dynamic_slice | solution.py:113
  73.5 1.1 %constant_dynamic-slice_fusion.2 = bf16[1,4,3,8,3,512]{5,1,0,3,2,4:T(4,128)(2,1)S(1)} fusion(bf16[16,4,3,8,3,512]{5,1,0,3,2,4:T(4,128)(2,1)} %get-tuple-element.185, s32[]{:T(128)} %get-tuple-element.174), kind=kLoop, calls=%fused_computation.22.clone.1 | loop fusion | bytes 589828 | tf_op jit(solution)/shard_map/while/body/jit(dynamic_index_in_dim)/dynamic_slice | solution.py:113
  75.4 2.3 %copy.34 = f32[8,64,16,4]{0,3,2,1:T(4,128)S(1)} copy(f32[8,64,16,4]{1,0,3,2:T(8,128)S(1)} %bitcast.83) | data formatting | bytes 262144 | tf_op jit(solution)/shard_map/transpose | solution.py:114
  78.4 19.0 %all_to_all.10 = f32[32,1,1024]{2,1,0:T(1,128)S(1)} all-to-all(f32[32,1,1024]{2,1,0:T(1,128)S(1)} %reshape.54), channel_id=1, replica_groups=mesh['elem'=32,'test'=8] {'elem'}, dimensions={0} | all-to-all | bytes 262144 | tf_op jit(solution)/shard_map/all_to_all | solution.py:38
  (107 shorter events, 17.6 us)
Async XLA Ops:
  2.3 6.2 %copy-start.2 = (f32[4,3]{1,0:T(4,128)S(1)}, f32[4,3]{1,0:T(4,128)}, u32[]{:S(2)}) copy-start(f32[4,3]{1,0:T(4,128)} %param.9) | copy-start | bytes 148
  2.3 6.3 %copy-start = (bf16[8,3,4096]{2,0,1:T(8,128)(2,1)S(1)}, bf16[8,3,4096]{2,0,1:T(8,128)(2,1)}, u32[]{:S(2)}) copy-start(bf16[8,3,4096]{2,0,1:T(8,128)(2,1)} %param.7) | copy-start | bytes 589828
  2.3 6.3 %copy-start.3 = (s32[8]{0:T(128)S(1)}, s32[8]{0:T(128)}, u32[]{:S(2)}) copy-start(s32[8]{0:T(128)} %param.8) | copy-start | bytes 100
  2.3 29.0 %all-to-all-start = ((bf16[8,8,3,4096]{3,1,2,0:T(8,128)(2,1)}), bf16[8,8,3,4096]{3,1,2,0:T(8,128)(2,1)S(1)}, u32[]{:S(2)}, u32[]{:S(2)}) async-start(bf16[8,8,3,4096]{3,1,2,0:T(8,128)(2,1)} %broadcast_in_dim.8), calls=%async_computation | async-start | bytes 3145728 | tf_op jit(solution)/shard_map/all_to_all | solution.py:21
  32.1 1.4 %copy-start.4 = (bf16[3,512,512,1,1]{2,1,4,3,0:T(8,128)(2,1)S(1)}, bf16[3,512,512,1,1]{2,1,4,3,0:T(8,128)(2,1)}, u32[]{:S(2)}) copy-start(bf16[3,512,512,1,1]{2,1,4,3,0:T(8,128)(2,1)} %constant.28) | copy-start | bytes 4718596
  37.8 7.7 %copy-start.1 = (f32[512]{0:T(512)S(1)}, f32[512]{0:T(512)}, u32[]{:S(2)}) copy-start(f32[512]{0:T(512)} %constant.23.clone) | copy-start | bytes 6148
where the time goes:
time: 102 us; the launch traced here: 99.7 us
  local copies, waits for them, and re-layouts  35 us (34%)
  waiting for transfers between devices  22.5 us (22%)
  blocking collectives  19 us (19%)
  matrix products  12.8 us (13%)
  starting transfers between devices  6.16 us (6%)
  other arithmetic  3.53 us (3%)
    all_to_all x1, waiting for transfers between devices, copy_for_each(): lax.all_to_all(jnp.broadcast_to(array[None], (peers, *array.shape)), axis...  22.5 us
    all_to_all x1, blocking collectives, sum_at_owner(): lax.all_to_all(in_blocks(array, dim, peers), axis, 0, 0, tiled=True)  19 us
    dynamic_slice x16, local copies, waits for them, and re-layouts, project(): result = lax.map(one_block, blocks)  17.2 us
    dot_general x16, matrix products, one_block(): jnp.einsum('ikedp,jdep->ijk', pairs, trial_fields, preferred_element_type...  8.49 us
    reshape x1, local copies, waits for them, and re-layouts, project(): grads.reshape((grad_modes // block_modes, block_modes) + grads.shape[1:])  7.72 us
    all_to_all x1, starting transfers between devices, copy_for_each(): lax.all_to_all(jnp.broadcast_to(array[None], (peers, *array.shape)), axis...  6.16 us
    dot_general x1, matrix products, gradient(): jnp.dot(flat, table, preferred_element_type=jnp.float32)  4.3 us
    transpose x1, local copies, waits for them, and re-layouts, project(): result.transpose(1, 2, 0, 3).reshape(test_modes, trial_modes, grad_modes)  2.3 us
  transfers between devices with their start and end apart: 1, of which 1 were waited for; matrix products, arithmetic and copies ran while one was open for 0% of the time, Pallas kernels for 0%

commit v1 on v0

v1 whole, which is shorter than its diff:
```python
import functools

import jax
import jax.numpy as jnp
import numpy as np
from jax import lax
from jax.experimental import pallas as pl
from jax.experimental.pallas import tpu as pltpu
from jax.sharding import Mesh, PartitionSpec as P

Q = 8
CUBE = Q**3
MODES = 64
LANES = 128
OWNERS = 16


def legendre_top(points, degree):
    before = points * 0.0 + 1.0
    current = points
    for order in range(2, degree + 1):
        following = ((2 * order - 1) * points * current - (order - 1) * before) / order
        before = current
        current = following
    return (current, before)


def lobatto_tables(order_points):
    degree = order_points - 1
    lobatto_nodes = np.cos(np.pi * np.arange(degree + 1) / degree)
    for sweep in range(100):
        top, lower = legendre_top(lobatto_nodes, degree)
        lobatto_nodes = lobatto_nodes - (lobatto_nodes * top - lower) / ((degree + 1) * top)
    lobatto_nodes = lobatto_nodes[::-1].copy()
    lobatto_nodes[0] = -1.0
    lobatto_nodes[-1] = 1.0
    values, unused = legendre_top(lobatto_nodes, degree)
    weights = 2.0 / (degree * (degree + 1) * values**2)
    identity = np.eye(order_points)
    distance = lobatto_nodes[:, None] - lobatto_nodes[None, :]
    spacing = np.where(identity > 0, 1.0, distance)
    derivative = np.where(identity > 0, 0.0, values[:, None] / values[None, :] / spacing)
    corner = degree * (degree + 1) / 4.0
    ends = np.concatenate([[-corner], np.zeros(degree - 1), [corner]])
    derivative = derivative + identity * ends[None, :]
    block_r = np.kron(np.eye(16), derivative)
    block_s = np.kron(np.eye(2), np.kron(derivative, identity))
    block_rs = np.concatenate([block_r.T, block_s.T], axis=1)
    along_t = np.kron(derivative, np.eye(order_points * order_points))
    cube_weights = np.kron(weights, np.kron(weights, weights))
    return (
        block_rs.astype(np.float32),
        along_t.T.astype(np.float32),
        cube_weights.astype(np.float32),
    )


def tensor_kernel(core_ref, x_ref, wq_ref, rs_ref, tt_ref, send_ref, own_ref, wide, grads, tests, prods):
    bf16 = jnp.bfloat16
    narrow = []
    high = (lax.broadcasted_iota(jnp.int32, (MODES, CUBE), 0) & 2) != 0
    swap = jnp.broadcast_to(core_ref[0], (MODES, CUBE)) != 0
    for c in range(3):
        rows = jnp.concatenate([x_ref[s, c].astype(jnp.float32) for s in range(8)], axis=0)
        turned = jnp.where(high, pltpu.roll(rows, 2, 0), pltpu.roll(rows, MODES - 2, 0))
        wide[c] = jnp.where(swap, turned, rows)
        narrow.append(rows.astype(bf16))
        tests[:, c * CUBE : (c + 1) * CUBE] = narrow[c]
    panel = jnp.concatenate(narrow, axis=0)
    along_t = jnp.dot(panel, tt_ref[...], preferred_element_type=jnp.float32)
    for b in range(CUBE // LANES):
        at = slice(b * LANES, (b + 1) * LANES)
        along_rs = jnp.dot(panel[:, at], rs_ref[...], preferred_element_type=jnp.float32)
        parts = (along_rs[:, :LANES], along_rs[:, LANES:], along_t[:, at])
        for d in range(3):
            scaled = (parts[d] * wq_ref[d : d + 1, at]).astype(bf16)
            for c in range(3):
                grads[c, d, :, at] = scaled[c * MODES : (c + 1) * MODES]
    for slot, out_ref in ((0, send_ref), (1, own_ref)):
        for pair in range(OWNERS // 2):
            hold = prods.at[pair % 2]
            trial = [
                4 * (2 * pair + a) + 2 * (1 - slot) + jj for a in range(2) for jj in range(2)
            ]
            for b in range(CUBE // LANES):
                at = slice(b * LANES, (b + 1) * LANES)
                fields = [
                    [
                        jnp.broadcast_to(wide[d, j : j + 1, at], (16, LANES)).astype(bf16)
                        for d in range(3)
                    ]
                    for j in trial
                ]
                for k in range(MODES // 16):
                    rows = slice(k * 16, (k + 1) * 16)
                    for c in range(3):
                        tile = [grads[c, d, rows, at] for d in range(3)]
                        for n in range(4):
                            f = fields[n]
                            value = f[0] * tile[0] + f[1] * tile[1] + f[2] * tile[2]
                            hold[
                                n * MODES + k * 16 : n * MODES + (k + 1) * 16,
                                c * CUBE + b * LANES : c * CUBE + (b + 1) * LANES,
                            ] = value
            result = lax.dot_general(
                tests[...], hold[...], (((1,), (1,)), ((), ())), preferred_element_type=jnp.float32
            )
            for a in range(2):
                block = result[:, a * LANES : (a + 1) * LANES]
                out_ref[2 * pair + a] = block.reshape(8, 8, LANES).astype(out_ref.dtype)


def local_tensor(core, fields, wq, block_rs, along_t, interpret=False):
    shape = (OWNERS, 8, 8, LANES)
    vmem = pl.BlockSpec(memory_space=pltpu.VMEM)
    return pl.pallas_call(
        tensor_kernel,
        out_shape=(
            jax.ShapeDtypeStruct(shape, jnp.bfloat16),
            jax.ShapeDtypeStruct(shape, jnp.bfloat16),
        ),
        in_specs=[pl.BlockSpec(memory_space=pltpu.SMEM), vmem, vmem, vmem, vmem],
        out_specs=(vmem, vmem),
        scratch_shapes=[
            pltpu.VMEM((3, MODES, CUBE), jnp.float32),
            pltpu.VMEM((3, 3, MODES, CUBE), jnp.bfloat16),
            pltpu.VMEM((MODES, 3 * CUBE), jnp.bfloat16),
            pltpu.VMEM((2, 4 * MODES, 3 * CUBE), jnp.bfloat16),
        ],
        compiler_params=pltpu.CompilerParams(vmem_limit_bytes=16 * 2**20),
        cost_estimate=pl.CostEstimate(flops=4 * 10**9, bytes_accessed=2**21, transcendentals=0),
        interpret=interpret,
        name="tensor",
    )(core, fields, wq, block_rs, along_t)


TEST = ("y_hi", "x")
REST = ("y_lo", "z", "y_hi", "x")


def body(mode_fields, elem_type, type_scales):
    bf16 = jnp.bfloat16
    block_rs, along_t, cube_weights = lobatto_tables(Q)
    block_rs = jnp.asarray(block_rs).astype(bf16)
    along_t = jnp.asarray(along_t).astype(bf16)
    total_points = CUBE * 256
    mine = lax.axis_index(TEST)
    kind = jnp.sum(jnp.where(jnp.arange(8, dtype=jnp.int32) == mine, elem_type, 0))
    picks = (jnp.arange(type_scales.shape[0], dtype=jnp.int32) == kind).astype(jnp.float32)
    scales = jnp.sum(picks[:, None] * type_scales, axis=0)
    wq = scales[:, None] * (jnp.asarray(cube_weights)[None, :] / jnp.prod(scales))
    pieces = mode_fields.reshape(8, 3, 8, CUBE).transpose(2, 1, 0, 3)
    fields = lax.all_to_all(pieces, TEST, 0, 0, tiled=True)
    core = lax.axis_index("core").astype(jnp.int32).reshape(1)
    send, own = local_tensor(core, fields, wq, block_rs, along_t)
    other = lax.ppermute(send, "core", [(0, 1), (1, 0)])
    both = (own.astype(jnp.float32) + other.astype(jnp.float32)).astype(bf16)
    chunks = lax.all_to_all(both.reshape(128, 8, LANES), REST, 0, 0, tiled=True)
    summed = jnp.sum(chunks.astype(jnp.float32), axis=0)
    return (summed * float(total_points) ** (-0.5)).reshape(8, 2, MODES)


def solution(mesh):
    split = Mesh(
        mesh.devices.reshape(2, 8, 2, 2, 4), ("y_lo", "z", "core", "y_hi", "x")
    )
    elem = ("y_lo", "z", "core")
    placed = (P(TEST, None, elem), P(elem), P())
    return jax.shard_map(
        body, mesh=split, in_specs=placed, out_specs=P(TEST, elem, None), check_vma=False
    )
```

time: 102 us -> 54.2 us (0.53); the launches traced: 99.7 us -> 53.9 us
  local copies, waits for them, and re-layouts: 35 us -> 3.02 us
  waiting for transfers between devices: 22.5 us -> 6.46 us
  matrix products: 12.8 us -> 0 us
  Pallas kernels: 0 us -> 8.64 us
  blocking collectives: 19 us -> 26.4 us
    all_to_all x1, waiting for transfers between devices: 22.5 us -> 4.94 us  [body(): fields = lax.all_to_all(pieces, TEST, 0, 0, tiled=True)]
    dynamic_slice x16 -> x0, local copies, waits for them, and re-layouts: 17.2 us -> none  [project(): result = lax.map(one_block, blocks)]
    dot_general x17 -> x0, matrix products: 12.8 us -> none  [the longest x16 8.49 us: one_block(): jnp.einsum('ikedp,jdep->ijk', pairs, trial_fields, preferred_element_type...]
    pallas_call x0 -> x1, Pallas kernels: none -> 8.64 us  [local_tensor(): pl.pallas_call(tensor_kernel, out_shape=(jax.ShapeDtypeStruct(shape, jnp....]
    all_to_all x1, blocking collectives: 19 us -> 26.4 us  [body(): chunks = lax.all_to_all(both.reshape(128, 8, LANES), REST, 0, 0, tiled=True)]
    reshape x1, local copies, waits for them, and re-layouts: 7.72 us -> 1.67 us  [body(): pieces = mode_fields.reshape(8, 3, 8, CUBE).transpose(2, 1, 0, 3)]
    transpose x2 -> x0, local copies, waits for them, and re-layouts: 2.88 us -> none  [the longest x1 2.3 us: project(): result.transpose(1, 2, 0, 3).reshape(test_modes, trial_modes, grad_modes)]
    broadcast_in_dim x1 -> x0, local copies, waits for them, and re-layouts: 2.25 us -> none  [copy_for_each(): jnp.broadcast_to(array[None], (peers, *array.shape))]
  transfers between devices with their start and end apart: 1 -> 2, of which waited for: 1 -> 2; matrix products, arithmetic and copies ran while one was open for 0% -> 5% of each run, Pallas kernels for 0% -> 0%
where the time goes in v1:
time: 54.2 us; the launch traced here: 53.9 us
  blocking collectives  26.4 us (49%)
  Pallas kernels  8.64 us (16%)
  waiting for transfers between devices  6.46 us (12%)
  starting transfers between devices  6.26 us (12%)
  local copies, waits for them, and re-layouts  3.02 us (6%)
  other arithmetic  3.01 us (6%)
    all_to_all x1, blocking collectives, body(): chunks = lax.all_to_all(both.reshape(128, 8, LANES), REST, 0, 0, tiled=True)  26.4 us
    pallas_call x1, Pallas kernels, local_tensor(): pl.pallas_call(tensor_kernel, out_shape=(jax.ShapeDtypeStruct(shape, jnp....  8.64 us
    all_to_all x1, starting transfers between devices, body(): fields = lax.all_to_all(pieces, TEST, 0, 0, tiled=True)  6.16 us
    all_to_all x1, waiting for transfers between devices, body(): fields = lax.all_to_all(pieces, TEST, 0, 0, tiled=True)  4.94 us
    reshape x1, local copies, waits for them, and re-layouts, body(): pieces = mode_fields.reshape(8, 3, 8, CUBE).transpose(2, 1, 0, 3)  1.67 us
    ppermute x1, waiting for transfers between devices, body(): other = lax.ppermute(send, 'core', [(0, 1), (1, 0)])  1.52 us
  transfers between devices with their start and end apart: 2, of which 2 were waited for; matrix products, arithmetic and copies ran while one was open for 5% of the time, Pallas kernels for 0%

profile of v1, /device:TPU:8, one launch (start us, length us, event | category | flops | bytes accessed | tf_op | source)
XLA Modules:
  0.0 53.9 jit_solution(13411615607715057803)
XLA Ops:
  0.0 0.0 copy-start
  0.0 1.7 %copy.10 = bf16[3,1,8,8,512]{4,3,1,0,2:T(8,128)(2,1)} copy(bf16[3,1,8,8,512]{4,3,2,1,0:T(8,128)(2,1)} %bitcast.10) | data formatting | bytes 393216 | tf_op jit(solution)/shard_map/reshape | solution.py:152
  1.7 0.0 copy-start.1
  1.7 6.2 %all-to-all-start = ((bf16[8,3,8,512]{3,2,1,0:T(8,128)(2,1)}), bf16[8,3,8,512]{3,2,1,0:T(8,128)(2,1)S(1)}, u32[]{:S(2)}, u32[]{:S(2)}) async-start(bf16[8,3,8,512]{3,2,1,0:T(8,128)(2,1)} %bitcast.8), calls=%async_computation | async-start | bytes 393216 | tf_op jit(solution)/shard_map/all_to_all | solution.py:153
  7.8 0.7 %copy-done.4 = s32[8]{0:T(128)S(1)} copy-done((s32[8]{0:T(128)S(1)}, s32[8]{0:T(128)}, u32[]{:S(2)}) %copy-start.4) | copy-done | bytes 56
  8.5 0.7 %fusion = s32[]{:T(128)} fusion(s32[8]{0:T(128)S(1)} %copy-done.4, s32[]{:T(128)S(6)} %add.6), kind=kLoop, calls=%fused_computation.9 | loop fusion | flops 23 | bytes 40 | tf_op jit(solution)/shard_map/reduce_sum | solution.py:148
  9.2 0.6 %compare_convert_fusion = f32[4]{0:T(128)S(1)} fusion(s32[]{:T(128)} %fusion), kind=kLoop, calls=%fused_computation.6 | loop fusion | flops 8 | bytes 20 | tf_op jit(solution)/shard_map/convert_element_type | solution.py:149
  9.8 0.0 copy-done.2
  9.8 0.0 copy-start.3
  9.8 0.1 multiply_reduce_fusion
  9.9 0.7 %reduce_prod.9 = f32[]{:T(128)} reduce(f32[3]{0:T(128)S(1)} %multiply_reduce_fusion, f32[]{:T(128)} %constant.26.clone.1), dimensions={0}, to_apply=%region_2.3 | reduce | flops 2 | bytes 20 | tf_op jit(solution)/shard_map/reduce_prod | solution.py:151
  10.6 0.0 copy-done.3
  10.6 0.6 %broadcast_divide_fusion = f32[512]{0:T(512)S(1)} fusion(f32[512]{0:T(512)S(1)} %copy-done.3, f32[]{:T(128)} %reduce_prod.9), kind=kLoop, calls=%fused_computation.8 | loop fusion | flops 512 | bytes 4100 | tf_op jit(solution)/shard_map/div | solution.py:151
  11.3 0.1 broadcast_multiply_fusion.wq_ref
  11.3 4.9 %all-to-all-done.x_ref = bf16[8,3,8,512]{3,2,1,0:T(8,128)(2,1)S(1)} async-done(((bf16[8,3,8,512]{3,2,1,0:T(8,128)(2,1)}), bf16[8,3,8,512]{3,2,1,0:T(8,128)(2,1)S(1)}, u32[]{:S(2)}, u32[]{:S(2)}) %all-to-all-start) | async-done | bytes 196640 | tf_op jit(solution)/shard_map/all_to_all | solution.py:153
  16.3 0.0 copy-done
  16.3 0.0 copy-done.1
  16.3 8.6 %tensor.1 = (bf16[16,8,8,128]{3,2,1,0:T(8,128)(2,1)S(1)}, bf16[16,8,8,128]{3,2,1,0:T(8,128)(2,1)S(1)}) custom-call(s32[1]{0:T(128)} %bitcast.core_ref, bf16[8,3,8,512]{3,2,1,0:T(8,128)(2,1)S(1)} %all-to-all-done.x_ref, f32[3,512]{1,0:T(4,128)S(1)} %broadcast_multiply_fusion.wq_ref, bf16[128,256]{1,0:T(8,128)(2,1)S(1)} %copy-done.1, bf16[512,512]{1,0:T(8,128)(2,1)S(1)} %copy-done), custom_call_target="tpu_custom_call" | custom-call | flops 4000000000 | bytes 2097152 | tf_op jit(solution)/shard_map/tensor/pallas_call | solution.py:116
  24.9 0.1 collective-permute-start
  25.0 1.5 %collective-permute-done = bf16[16,8,8,128]{3,2,1,0:T(8,128)(2,1)S(1)} collective-permute-done((bf16[16,8,8,128]{3,2,1,0:T(8,128)(2,1)S(1)}, bf16[16,8,8,128]{3,2,1,0:T(8,128)(2,1)S(1)}, u32[]{:S(2)}, u32[]{:S(2)}) %collective-permute-start) | collective-permute-done | bytes 262176 | tf_op jit(solution)/shard_map/ppermute | solution.py:156
  26.5 0.1 add_convert_fusion
  26.6 26.4 %all_to_all.10 = bf16[128,8,128]{2,1,0:T(8,128)(2,1)S(1)} all-to-all(bf16[128,8,128]{2,1,0:T(8,128)(2,1)S(1)} %bitcast.9), channel_id=1, replica_groups=mesh['y_lo'=2,'z'=8,'core'=2,'y_hi'=2,'x'=4] {'y_lo','z','y_hi','x'}, dimensions={0} | all-to-all | bytes 524288 | tf_op jit(solution)/shard_map/all_to_all | solution.py:158
  53.1 0.1 convert_reduce_fusion
  53.2 0.7 %mul.42 = f32[8,2,64]{2,1,0:T(2,128)} reshape(f32[8,128]{1,0:T(8,128)S(1)} %broadcast_multiply_fusion.1) | data formatting | bytes 8192 | tf_op jit(solution)/shard_map/mul | solution.py:160
  (3 shorter events, 0.0 us)
Async XLA Ops:
  0.0 16.3 %copy-start = (bf16[512,512]{1,0:T(8,128)(2,1)S(1)}, bf16[512,512]{1,0:T(8,128)(2,1)}, u32[]{:S(2)}) copy-start(bf16[512,512]{1,0:T(8,128)(2,1)} %constant.33.tt_ref) | copy-start | bytes 1572868
  1.7 14.6 %copy-start.1 = (bf16[128,256]{1,0:T(8,128)(2,1)S(1)}, bf16[128,256]{1,0:T(8,128)(2,1)}, u32[]{:S(2)}) copy-start(bf16[128,256]{1,0:T(8,128)(2,1)} %constant.32.rs_ref) | copy-start | bytes 196612
  1.7 14.6 %all-to-all-start = ((bf16[8,3,8,512]{3,2,1,0:T(8,128)(2,1)}), bf16[8,3,8,512]{3,2,1,0:T(8,128)(2,1)S(1)}, u32[]{:S(2)}, u32[]{:S(2)}) async-start(bf16[8,3,8,512]{3,2,1,0:T(8,128)(2,1)} %bitcast.8), calls=%async_computation | async-start | bytes 393216 | tf_op jit(solution)/shard_map/all_to_all | solution.py:153
  7.8 0.7 %copy-start.4 = (s32[8]{0:T(128)S(1)}, s32[8]{0:T(128)}, u32[]{:S(2)}) copy-start(s32[8]{0:T(128)} %param.7) | copy-start | bytes 100
  8.5 1.3 %copy-start.2 = (f32[4,3]{1,0:T(4,128)S(1)}, f32[4,3]{1,0:T(4,128)}, u32[]{:S(2)}) copy-start(f32[4,3]{1,0:T(4,128)} %param.8) | copy-start | bytes 148
  9.8 0.8 %copy-start.3 = (f32[512]{0:T(512)S(1)}, f32[512]{0:T(512)}, u32[]{:S(2)}) copy-start(f32[512]{0:T(512)} %constant.30.clone) | copy-start | bytes 6148
  24.9 1.6 %collective-permute-start = (bf16[16,8,8,128]{3,2,1,0:T(8,128)(2,1)S(1)}, bf16[16,8,8,128]{3,2,1,0:T(8,128)(2,1)S(1)}, u32[]{:S(2)}, u32[]{:S(2)}) collective-permute-start(bf16[16,8,8,128]{3,2,1,0:T(8,128)(2,1)S(1)} %get-tuple-element.8), channel_id=1, source_target_pairs={{0,8},{8,0},{1,9},{9,1},{2,10},{10,2},{3,11},{11,3},{4,12},{12,4},... | collective-permute-start | bytes 786440 | tf_op jit(solution)/shard_map/ppermute | solution.py:156

commit v2 on v1

v2 whole, which is shorter than its diff:
```python
import functools

import jax
import jax.numpy as jnp
import numpy as np
from jax import lax
from jax.experimental import pallas as pl
from jax.experimental.pallas import tpu as pltpu
from jax.sharding import Mesh, PartitionSpec as P

Q = 8
CUBE = Q**3
MODES = 64
LANES = 128
OWNERS = 16
TEST = ("y_hi", "x")


def legendre_top(points, degree):
    before = points * 0.0 + 1.0
    current = points
    for order in range(2, degree + 1):
        following = ((2 * order - 1) * points * current - (order - 1) * before) / order
        before = current
        current = following
    return (current, before)


def lobatto_tables(order_points):
    degree = order_points - 1
    lobatto_nodes = np.cos(np.pi * np.arange(degree + 1) / degree)
    for sweep in range(100):
        top, lower = legendre_top(lobatto_nodes, degree)
        lobatto_nodes = lobatto_nodes - (lobatto_nodes * top - lower) / ((degree + 1) * top)
    lobatto_nodes = lobatto_nodes[::-1].copy()
    lobatto_nodes[0] = -1.0
    lobatto_nodes[-1] = 1.0
    values, unused = legendre_top(lobatto_nodes, degree)
    weights = 2.0 / (degree * (degree + 1) * values**2)
    identity = np.eye(order_points)
    distance = lobatto_nodes[:, None] - lobatto_nodes[None, :]
    spacing = np.where(identity > 0, 1.0, distance)
    derivative = np.where(identity > 0, 0.0, values[:, None] / values[None, :] / spacing)
    corner = degree * (degree + 1) / 4.0
    ends = np.concatenate([[-corner], np.zeros(degree - 1), [corner]])
    derivative = derivative + identity * ends[None, :]
    block_r = np.kron(np.eye(16), derivative)
    block_s = np.kron(np.eye(2), np.kron(derivative, identity))
    block_rs = np.concatenate([block_r.T, block_s.T], axis=1)
    along_t = np.kron(derivative, np.eye(order_points * order_points))
    cube_weights = np.kron(weights, np.kron(weights, weights))
    return (
        block_rs.astype(np.float32),
        along_t.T.astype(np.float32),
        cube_weights.astype(np.float32),
    )


def tensor_kernel(
    kinds_ref, types_ref, weights_ref, x_ref, rs_ref, tt_ref, send_ref, own_ref, wide, grads, tests
):
    bf16 = jnp.bfloat16
    f32 = jnp.float32
    blocks = CUBE // LANES
    core = lax.axis_index("core")
    mine = lax.axis_index(TEST)
    kinds = kinds_ref[...]
    here = lax.broadcasted_iota(jnp.int32, kinds.shape, 1) == mine
    kind = jnp.sum(jnp.where(here, kinds.astype(f32), 0.0), axis=1, keepdims=True)
    table = types_ref[...]
    picked = lax.broadcasted_iota(jnp.int32, table.shape, 0).astype(f32) == kind
    scales = jnp.sum(jnp.where(picked, table, 0.0), axis=0, keepdims=True)
    along = [scales[:, d : d + 1] for d in range(3)]
    quad = weights_ref[...] / (along[0] * along[1] * along[2])
    high = (lax.broadcasted_iota(jnp.int32, (MODES, CUBE), 0) & 2) != 0
    swap = jnp.broadcast_to(core, (MODES, CUBE)) != 0
    narrow = []
    for c in range(3):
        rows = jnp.concatenate([x_ref[s, c].astype(f32) for s in range(8)], axis=0)
        turned = jnp.where(high, pltpu.roll(rows, 2, 0), pltpu.roll(rows, MODES - 2, 0))
        turned = jnp.where(swap, turned, rows)
        weighted = rows * quad
        upper = weighted.astype(bf16)
        lower = (weighted - upper.astype(f32)).astype(bf16)
        for b in range(blocks):
            at = slice(b * LANES, (b + 1) * LANES)
            wide[c, b] = turned[:, at]
            tests[c * blocks + b, :MODES] = upper[:, at]
            tests[c * blocks + b, MODES:] = lower[:, at]
        narrow.append(rows.astype(bf16))
    panel = jnp.concatenate(narrow, axis=0)
    along_t = jnp.dot(panel, tt_ref[...], preferred_element_type=f32)
    for b in range(blocks):
        at = slice(b * LANES, (b + 1) * LANES)
        along_rs = jnp.dot(panel[:, at], rs_ref[...], preferred_element_type=f32)
        parts = (along_rs[:, :LANES], along_rs[:, LANES:], along_t[:, at])
        for d in range(3):
            scaled = (parts[d] * along[d]).astype(bf16)
            for c in range(3):
                grads[c, d, b] = scaled[c * MODES : (c + 1) * MODES]
    for slot, out_ref in ((0, send_ref), (1, own_ref)):
        for pair in range(OWNERS // 2):
            made = {}
            trial = [
                4 * (2 * pair + a) + 2 * (1 - slot) + jj for a in range(2) for jj in range(2)
            ]
            for b in range(blocks):
                fields = [
                    [
                        jnp.broadcast_to(wide[d, b, j : j + 1], (16, LANES)).astype(bf16)
                        for d in range(3)
                    ]
                    for j in trial
                ]
                for k in range(MODES // 16):
                    rows = slice(k * 16, (k + 1) * 16)
                    for c in range(3):
                        tile = [grads[c, d, b, rows] for d in range(3)]
                        for n in range(4):
                            f = fields[n]
                            value = f[0] * tile[0] + f[1] * tile[1] + f[2] * tile[2]
                            made[c * blocks + b, n, k] = value
            left = jnp.concatenate([tests[n] for n in range(3 * blocks)], axis=1)
            right = jnp.concatenate(
                [
                    jnp.concatenate(
                        [made[m, n, k] for n in range(4) for k in range(MODES // 16)], axis=0
                    )
                    for m in range(3 * blocks)
                ],
                axis=1,
            )
            both = lax.dot_general(
                left, right, (((1,), (1,)), ((), ())), preferred_element_type=f32
            )
            result = both[:MODES] + both[MODES:]
            for a in range(2):
                block = result[:, a * LANES : (a + 1) * LANES]
                out_ref[2 * pair + a] = block.reshape(8, 8, LANES).astype(out_ref.dtype)


def local_tensor(kinds, types, weights, fields, block_rs, along_t, interpret=False):
    shape = (OWNERS, 8, 8, LANES)
    blocks = CUBE // LANES
    vmem = pl.BlockSpec(memory_space=pltpu.VMEM)
    return pl.pallas_call(
        tensor_kernel,
        out_shape=(
            jax.ShapeDtypeStruct(shape, jnp.bfloat16),
            jax.ShapeDtypeStruct(shape, jnp.float32),
        ),
        in_specs=[vmem] * 6,
        out_specs=(vmem, vmem),
        scratch_shapes=[
            pltpu.VMEM((3, blocks, MODES, LANES), jnp.float32),
            pltpu.VMEM((3, 3, blocks, MODES, LANES), jnp.bfloat16),
            pltpu.VMEM((3 * blocks, 2 * MODES, LANES), jnp.bfloat16),
        ],
        compiler_params=pltpu.CompilerParams(vmem_limit_bytes=16 * 2**20),
        cost_estimate=pl.CostEstimate(flops=4 * 10**9, bytes_accessed=2**21, transcendentals=0),
        interpret=interpret,
        name="tensor",
    )(kinds, types, weights, fields, block_rs, along_t)


REST = ("y_lo", "z", "y_hi", "x")


def body(mode_fields, elem_type, type_scales):
    bf16 = jnp.bfloat16
    block_rs, along_t, cube_weights = lobatto_tables(Q)
    block_rs = jnp.asarray(block_rs).astype(bf16)
    along_t = jnp.asarray(along_t).astype(bf16)
    total_points = CUBE * 256
    pieces = mode_fields.reshape(8, 3, 8, CUBE).transpose(2, 1, 0, 3)
    fields = lax.all_to_all(pieces, TEST, 0, 0, tiled=True)
    send, own = local_tensor(
        elem_type.reshape(1, 8), type_scales, jnp.asarray(cube_weights)[None], fields, block_rs, along_t
    )
    other = lax.ppermute(send, "core", [(0, 1), (1, 0)])
    both = (own + other.astype(jnp.float32)).astype(bf16)
    chunks = lax.all_to_all(both.reshape(128, 8, LANES), REST, 0, 0, tiled=True)
    summed = jnp.sum(chunks.astype(jnp.float32), axis=0)
    return (summed * float(total_points) ** (-0.5)).reshape(8, 2, MODES)


def solution(mesh):
    split = Mesh(
        mesh.devices.reshape(2, 8, 2, 2, 4), ("y_lo", "z", "core", "y_hi", "x")
    )
    elem = ("y_lo", "z", "core")
    placed = (P(TEST, None, elem), P(elem), P())
    return jax.shard_map(
        body, mesh=split, in_specs=placed, out_specs=P(TEST, elem, None), check_vma=False
    )
```

time: 54.2 us -> 50.1 us (0.924)
  blocking collectives: 26.4 us -> 40.8 us
  starting transfers between devices: 6.26 us -> 0.09 us
  waiting for transfers between devices: 6.46 us -> 1.52 us
  Pallas kernels: 8.64 us -> 4.8 us
  other arithmetic: 3.01 us -> 0.22 us
  local copies, waits for them, and re-layouts: 3.02 us -> 2.33 us
    all_to_all x0 -> x1, blocking collectives: none -> 14.4 us  [body(): fields = lax.all_to_all(pieces, TEST, 0, 0, tiled=True)]
    all_to_all x1 -> x0, starting transfers between devices: 6.16 us -> none  [body(): fields = lax.all_to_all(pieces, TEST, 0, 0, tiled=True)]
    all_to_all x1 -> x0, waiting for transfers between devices: 4.94 us -> none  [body(): fields = lax.all_to_all(pieces, TEST, 0, 0, tiled=True)]
    pallas_call x1, Pallas kernels: 8.64 us -> 4.8 us  [local_tensor(): pl.pallas_call(tensor_kernel, out_shape=(jax.ShapeDtypeStruct(shape, jnp....]
    reduce_sum x2 -> x0, other arithmetic: 0.78 us -> none  [the longest x1 0.69 us: body(): jnp.sum(jnp.where(jnp.arange(8, dtype=jnp.int32) == mine, elem_type, 0))]
    reduce_prod x1 -> x0, other arithmetic: 0.7 us -> none  [body(): jnp.prod(scales)]
    reshape x1, local copies, waits for them, and re-layouts: 1.67 us -> 1 us  [body(): pieces = mode_fields.reshape(8, 3, 8, CUBE).transpose(2, 1, 0, 3)]
    div x1 -> x0, other arithmetic: 0.62 us -> none  [body(): jnp.asarray(cube_weights)[None, :] / jnp.prod(scales)]
  transfers between devices with their start and end apart: 2 -> 1, of which waited for: 2 -> 1; matrix products, arithmetic and copies ran while one was open for 5% -> 0% of each run, Pallas kernels for 0% -> 0%
where the time goes in v2:
time: 50.1 us; the launch traced here: 49.9 us
  blocking collectives  40.8 us (81%)
  Pallas kernels  4.8 us (10%)
  local copies, waits for them, and re-layouts  2.33 us (5%)
  waiting for transfers between devices  1.52 us (3%)
    all_to_all x1, blocking collectives, body(): chunks = lax.all_to_all(both.reshape(128, 8, LANES), REST, 0, 0, tiled=True)  26.4 us
    all_to_all x1, blocking collectives, body(): fields = lax.all_to_all(pieces, TEST, 0, 0, tiled=True)  14.4 us
    pallas_call x1, Pallas kernels, local_tensor(): pl.pallas_call(tensor_kernel, out_shape=(jax.ShapeDtypeStruct(shape, jnp....  4.8 us
    ppermute x1, waiting for transfers between devices, body(): other = lax.ppermute(send, 'core', [(0, 1), (1, 0)])  1.52 us
  transfers between devices with their start and end apart: 1, of which 1 were waited for; matrix products, arithmetic and copies ran while one was open for 0% of the time, Pallas kernels for 0%

profile of v2, /device:TPU:8, one launch (start us, length us, event | category | flops | bytes accessed | tf_op | source)
XLA Modules:
  0.0 49.9 jit_solution(18372215012131241053)
XLA Ops:
  0.0 0.0 copy-start.2
  0.0 1.0 %copy.10 = bf16[3,1,8,8,512]{4,3,1,0,2:T(8,128)(2,1)S(1)} copy(bf16[3,1,8,8,512]{4,3,2,1,0:T(8,128)(2,1)} %bitcast.12) | data formatting | bytes 393216 | tf_op jit(solution)/shard_map/reshape | solution.py:175
  1.0 0.0 copy-start
  1.0 0.0 copy-start.3
  1.0 0.0 copy-start.4
  1.0 14.4 %all_to_all.10.x_ref = bf16[8,3,8,512]{3,2,1,0:T(8,128)(2,1)S(1)} all-to-all(bf16[8,3,8,512]{3,2,1,0:T(8,128)(2,1)S(1)} %bitcast.11), channel_id=1, replica_groups=mesh['y_lo'=2,'z'=8,'core'=2,'y_hi'=2,'x'=4] {'y_hi','x'}, dimensions={0} | all-to-all | bytes 393216 | tf_op jit(solution)/shard_map/all_to_all | solution.py:176
  15.4 0.0 copy-start.1
  15.4 0.0 copy-done.2
  15.4 0.0 copy-done
  15.4 0.0 copy-done.3
  15.5 0.0 copy-done.4
  15.5 0.6 %copy-done.1 = s32[8]{0:T(128)S(1)} copy-done((s32[8]{0:T(128)S(1)}, s32[8]{0:T(128)}, u32[]{:S(2)}) %copy-start.1) | copy-done | bytes 56
  16.1 4.8 %tensor.1 = (bf16[16,8,8,128]{3,2,1,0:T(8,128)(2,1)S(1)}, f32[16,8,8,128]{3,2,1,0:T(8,128)S(1)}) custom-call(s32[1,8]{1,0:T(1,128)S(1)} %bitcast.9, f32[4,3]{1,0:T(4,128)S(1)} %copy-done, f32[1,512]{1,0:T(1,128)S(1)} %copy-done.4, bf16[8,3,8,512]{3,2,1,0:T(8,128)(2,1)S(1)} %all_to_all.10.x_ref, bf16[128,256]{1,0:T(8,128)(2,1)S(1)} %copy-done.3, ...), custom_call_target="tpu_custom_call" | custom-call | flops 4000000000 | bytes 2097152 | tf_op jit(solution)/shard_map/tensor/pallas_call | solution.py:146
  20.9 0.1 collective-permute-start
  21.0 1.5 %collective-permute-done = bf16[16,8,8,128]{3,2,1,0:T(8,128)(2,1)S(1)} collective-permute-done((bf16[16,8,8,128]{3,2,1,0:T(8,128)(2,1)S(1)}, bf16[16,8,8,128]{3,2,1,0:T(8,128)(2,1)S(1)}, u32[]{:S(2)}, u32[]{:S(2)}) %collective-permute-start) | collective-permute-done | bytes 262176 | tf_op jit(solution)/shard_map/ppermute | solution.py:180
  22.5 0.1 add_convert_fusion
  22.6 26.4 %all_to_all.11 = bf16[128,8,128]{2,1,0:T(8,128)(2,1)S(1)} all-to-all(bf16[128,8,128]{2,1,0:T(8,128)(2,1)S(1)} %bitcast.10), channel_id=1, replica_groups=mesh['y_lo'=2,'z'=8,'core'=2,'y_hi'=2,'x'=4] {'y_lo','z','y_hi','x'}, dimensions={0} | all-to-all | bytes 524288 | tf_op jit(solution)/shard_map/all_to_all | solution.py:182
  49.0 0.1 convert_reduce_fusion
  49.2 0.7 %mul.12 = f32[8,2,64]{2,1,0:T(2,128)} reshape(f32[8,128]{1,0:T(8,128)S(1)} %broadcast_multiply_fusion) | data formatting | bytes 8192 | tf_op jit(solution)/shard_map/mul | solution.py:184
  (1 shorter events, 0.0 us)
Async XLA Ops:
  0.0 15.4 %copy-start.2 = (bf16[512,512]{1,0:T(8,128)(2,1)S(1)}, bf16[512,512]{1,0:T(8,128)(2,1)}, u32[]{:S(2)}) copy-start(bf16[512,512]{1,0:T(8,128)(2,1)} %constant.16.tt_ref) | copy-start | bytes 1572868
  1.0 14.4 %copy-start = (f32[4,3]{1,0:T(4,128)S(1)}, f32[4,3]{1,0:T(4,128)}, u32[]{:S(2)}) copy-start(f32[4,3]{1,0:T(4,128)} %types_ref.1) | copy-start | bytes 148
  1.0 14.4 %copy-start.3 = (bf16[128,256]{1,0:T(8,128)(2,1)S(1)}, bf16[128,256]{1,0:T(8,128)(2,1)}, u32[]{:S(2)}) copy-start(bf16[128,256]{1,0:T(8,128)(2,1)} %constant.15.rs_ref) | copy-start | bytes 196612
  1.0 14.4 %copy-start.4 = (f32[1,512]{1,0:T(1,128)S(1)}, f32[1,512]{1,0:T(1,128)}, u32[]{:S(2)}) copy-start(f32[1,512]{1,0:T(1,128)} %constant.14.weights_ref) | copy-start | bytes 6148
  15.4 0.7 %copy-start.1 = (s32[8]{0:T(128)S(1)}, s32[8]{0:T(128)}, u32[]{:S(2)}) copy-start(s32[8]{0:T(128)} %param.7) | copy-start | bytes 100
  20.9 1.6 %collective-permute-start = (bf16[16,8,8,128]{3,2,1,0:T(8,128)(2,1)S(1)}, bf16[16,8,8,128]{3,2,1,0:T(8,128)(2,1)S(1)}, u32[]{:S(2)}, u32[]{:S(2)}) collective-permute-start(bf16[16,8,8,128]{3,2,1,0:T(8,128)(2,1)S(1)} %get-tuple-element.8), channel_id=1, source_target_pairs={{0,8},{8,0},{1,9},{9,1},{2,10},{10,2},{3,11},{11,3},{4,12},{12,4},... | collective-permute-start | bytes 786440 | tf_op jit(solution)/shard_map/ppermute | solution.py:180

commit v3 on v2

--- a/solution.py
+++ b/solution.py
@@ -56,20 +56,56 @@
     )
 
 
-def tensor_kernel(
-    kinds_ref, types_ref, weights_ref, x_ref, rs_ref, tt_ref, send_ref, own_ref, wide, grads, tests
-):
+def contract(slot, out_ref, wide, grads, tests):
+    bf16 = jnp.bfloat16
+    f32 = jnp.float32
+    blocks = CUBE // LANES
+    for pair in range(OWNERS // 2):
+        made = {}
+        trial = [4 * (2 * pair + a) + 2 * (1 - slot) + jj for a in range(2) for jj in range(2)]
+        for b in range(blocks):
+            fields = [
+                [
+                    jnp.broadcast_to(wide[d, b, j : j + 1], (16, LANES)).astype(bf16)
+                    for d in range(3)
+                ]
+                for j in trial
+            ]
+            for k in range(MODES // 16):
+                rows = slice(k * 16, (k + 1) * 16)
+                for c in range(3):
+                    tile = [grads[c, d, b, rows] for d in range(3)]
+                    for n in range(4):
+                        f = fields[n]
+                        value = f[0] * tile[0] + f[1] * tile[1] + f[2] * tile[2]
+                        made[c * blocks + b, n, k] = value
+        left = jnp.concatenate([tests[n] for n in range(3 * blocks)], axis=1)
+        right = jnp.concatenate(
+            [
+                jnp.concatenate(
+                    [made[m, n, k] for n in range(4) for k in range(MODES // 16)], axis=0
+                )
+                for m in range(3 * blocks)
+            ],
+            axis=1,
+        )
+        both = lax.dot_general(left, right, (((1,), (1,)), ((), ())), preferred_element_type=f32)
+        result = both[:MODES] + both[MODES:]
+        for a in range(2):
+            block = result[:, a * LANES : (a + 1) * LANES]
+            out_ref[2 * pair + a] = block.reshape(8, 8, LANES).astype(out_ref.dtype)
+
+
+def first_kernel(kinds_ref, types_ref, weights_ref, x_ref, rs_ref, tt_ref, send_ref, wide, grads, tests):
     bf16 = jnp.bfloat16
     f32 = jnp.float32
     blocks = CUBE // LANES
     core = lax.axis_index("core")
-    mine = lax.axis_index(TEST)
-    kinds = kinds_ref[...]
-    here = lax.broadcasted_iota(jnp.int32, kinds.shape, 1) == mine
+    kinds = kinds_ref[...].reshape(1, 8)
+    here = lax.broadcasted_iota(jnp.int32, (1, 8), 1) == lax.axis_index(TEST)
     kind = jnp.sum(jnp.where(here, kinds.astype(f32), 0.0), axis=1, keepdims=True)
-    table = types_ref[...]
-    picked = lax.broadcasted_iota(jnp.int32, table.shape, 0).astype(f32) == kind
-    scales = jnp.sum(jnp.where(picked, table, 0.0), axis=0, keepdims=True)
+    picked = lax.broadcasted_iota(jnp.int32, (4, 3), 0).astype(f32) == kind
+    scales = jnp.sum(jnp.where(picked, types_ref[...], 0.0), axis=0, keepdims=True)
     along = [scales[:, d : d + 1] for d in range(3)]
     quad = weights_ref[...] / (along[0] * along[1] * along[2])
     high = (lax.broadcasted_iota(jnp.int32, (MODES, CUBE), 0) & 2) != 0
@@ -98,69 +134,46 @@
             scaled = (parts[d] * along[d]).astype(bf16)
             for c in range(3):
                 grads[c, d, b] = scaled[c * MODES : (c + 1) * MODES]
-    for slot, out_ref in ((0, send_ref), (1, own_ref)):
-        for pair in range(OWNERS // 2):
-            made = {}
-            trial = [
-                4 * (2 * pair + a) + 2 * (1 - slot) + jj for a in range(2) for jj in range(2)
-            ]
-            for b in range(blocks):
-                fields = [
-                    [
-                        jnp.broadcast_to(wide[d, b, j : j + 1], (16, LANES)).astype(bf16)
-                        for d in range(3)
-                    ]
-                    for j in trial
-                ]
-                for k in range(MODES // 16):
-                    rows = slice(k * 16, (k + 1) * 16)
-                    for c in range(3):
-                        tile = [grads[c, d, b, rows] for d in range(3)]
-                        for n in range(4):
-                            f = fields[n]
-                            value = f[0] * tile[0] + f[1] * tile[1] + f[2] * tile[2]
-                            made[c * blocks + b, n, k] = value
-            left = jnp.concatenate([tests[n] for n in range(3 * blocks)], axis=1)
-            right = jnp.concatenate(
-                [
-                    jnp.concatenate(
-                        [made[m, n, k] for n in range(4) for k in range(MODES // 16)], axis=0
-                    )
-                    for m in range(3 * blocks)
-                ],
-                axis=1,
-            )
-            both = lax.dot_general(
-                left, right, (((1,), (1,)), ((), ())), preferred_element_type=f32
-            )
-            result = both[:MODES] + both[MODES:]
-            for a in range(2):
-                block = result[:, a * LANES : (a + 1) * LANES]
-                out_ref[2 * pair + a] = block.reshape(8, 8, LANES).astype(out_ref.dtype)
-
-
-def local_tensor(kinds, types, weights, fields, block_rs, along_t, interpret=False):
-    shape = (OWNERS, 8, 8, LANES)
+    contract(0, send_ref, wide, grads, tests)
+
+
+def second_kernel(wide, grads, tests, own_ref):
+    contract(1, own_ref, wide, grads, tests)
+
+
+SHAPE = (OWNERS, 8, 8, LANES)
+
+
+def first_half(kinds, types, weights, fields, block_rs, along_t):
     blocks = CUBE // LANES
     vmem = pl.BlockSpec(memory_space=pltpu.VMEM)
     return pl.pallas_call(
-        tensor_kernel,
+        first_kernel,
         out_shape=(
-            jax.ShapeDtypeStruct(shape, jnp.bfloat16),
-            jax.ShapeDtypeStruct(shape, jnp.float32),
+            jax.ShapeDtypeStruct(SHAPE, jnp.bfloat16),
+            jax.ShapeDtypeStruct((3, blocks, MODES, LANES), jnp.float32),
+            jax.ShapeDtypeStruct((3, 3, blocks, MODES, LANES), jnp.bfloat16),
+            jax.ShapeDtypeStruct((3 * blocks, 2 * MODES, LANES), jnp.bfloat16),
         ),
         in_specs=[vmem] * 6,
-        out_specs=(vmem, vmem),
-        scratch_shapes=[
-            pltpu.VMEM((3, blocks, MODES, LANES), jnp.float32),
-            pltpu.VMEM((3, 3, blocks, MODES, LANES), jnp.bfloat16),
-            pltpu.VMEM((3 * blocks, 2 * MODES, LANES), jnp.bfloat16),
-        ],
+        out_specs=(vmem,) * 4,
         compiler_params=pltpu.CompilerParams(vmem_limit_bytes=16 * 2**20),
-        cost_estimate=pl.CostEstimate(flops=4 * 10**9, bytes_accessed=2**21, transcendentals=0),
-        interpret=interpret,
-        name="tensor",
+        cost_estimate=pl.CostEstimate(flops=3 * 10**9, bytes_accessed=2**21, transcendentals=0),
+        name="first",
     )(kinds, types, weights, fields, block_rs, along_t)
+
+
+def second_half(wide, grads, tests):
+    vmem = pl.BlockSpec(memory_space=pltpu.VMEM)
+    return pl.pallas_call(
+        second_kernel,
+        out_shape=jax.ShapeDtypeStruct(SHAPE, jnp.float32),
+        in_specs=[vmem] * 3,
+        out_specs=vmem,
+        compiler_params=pltpu.CompilerParams(vmem_limit_bytes=16 * 2**20),
+        cost_estimate=pl.CostEstimate(flops=2 * 10**9, bytes_accessed=2**21, transcendentals=0),
+        name="second",
+    )(wide, grads, tests)
 
 
 REST = ("y_lo", "z", "y_hi", "x")
@@ -174,10 +187,11 @@
     total_points = CUBE * 256
     pieces = mode_fields.reshape(8, 3, 8, CUBE).transpose(2, 1, 0, 3)
     fields = lax.all_to_all(pieces, TEST, 0, 0, tiled=True)
-    send, own = local_tensor(
-        elem_type.reshape(1, 8), type_scales, jnp.asarray(cube_weights)[None], fields, block_rs, along_t
+    send, wide, grads, tests = first_half(
+        elem_type, type_scales, jnp.asarray(cube_weights)[None], fields, block_rs, along_t
     )
     other = lax.ppermute(send, "core", [(0, 1), (1, 0)])
+    own = second_half(wide, grads, tests)
     both = (own + other.astype(jnp.float32)).astype(bf16)
     chunks = lax.all_to_all(both.reshape(128, 8, LANES), REST, 0, 0, tiled=True)
     summed = jnp.sum(chunks.astype(jnp.float32), axis=0)

time: 50.1 us -> 48.4 us (0.966)
  waiting for transfers between devices: 1.52 us -> 0.01 us
  local copies, waits for them, and re-layouts: 2.33 us -> 1.71 us
    ppermute x1, waiting for transfers between devices: 1.52 us -> 0.01 us  [body(): other = lax.ppermute(send, 'core', [(0, 1), (1, 0)])]
    unnamed x10, local copies, waits for them, and re-layouts: 0.66 us -> 0.03 us
    pallas_call x1 -> x2, Pallas kernels: 4.8 us -> 4.94 us  [the longest x1 2.7 us: first_half(): pl.pallas_call(first_kernel, out_shape=(jax.ShapeDtypeStruct(SHAPE, jnp.b...]
  transfers between devices with their start and end apart: 1 -> 1, of which waited for: 1 -> 0; matrix products, arithmetic and copies ran while one was open for 0% -> 0% of each run, Pallas kernels for 0% -> 5%
where the time goes in v3:
time: 48.4 us; the launch traced here: 48.2 us
  blocking collectives  41.2 us (85%)
  Pallas kernels  4.94 us (10%)
  local copies, waits for them, and re-layouts  1.71 us (4%)
    all_to_all x1, blocking collectives, body(): chunks = lax.all_to_all(both.reshape(128, 8, LANES), REST, 0, 0, tiled=True)  26.8 us
    all_to_all x1, blocking collectives, body(): fields = lax.all_to_all(pieces, TEST, 0, 0, tiled=True)  14.4 us
    pallas_call x1, Pallas kernels, first_half(): pl.pallas_call(first_kernel, out_shape=(jax.ShapeDtypeStruct(SHAPE, jnp.b...  2.7 us
    pallas_call x1, Pallas kernels, second_half(): pl.pallas_call(second_kernel, out_shape=jax.ShapeDtypeStruct(SHAPE, jnp.f...  2.25 us
    reshape x1, local copies, waits for them, and re-layouts, body(): pieces = mode_fields.reshape(8, 3, 8, CUBE).transpose(2, 1, 0, 3)  1 us
  transfers between devices with their start and end apart: 1, of which 0 were waited for; matrix products, arithmetic and copies ran while one was open for 0% of the time, Pallas kernels for 5%

profile of v3, /device:TPU:8, one launch (start us, length us, event | category | flops | bytes accessed | tf_op | source)
XLA Modules:
  0.0 48.2 jit_solution(4497074152657796236)
XLA Ops:
  0.0 0.0 copy-start.2
  0.0 1.0 %copy.10 = bf16[3,1,8,8,512]{4,3,1,0,2:T(8,128)(2,1)S(1)} copy(bf16[3,1,8,8,512]{4,3,2,1,0:T(8,128)(2,1)} %bitcast.10) | data formatting | bytes 393216 | tf_op jit(solution)/shard_map/reshape | solution.py:188
  1.0 0.0 copy-start
  1.0 0.0 copy-start.1
  1.0 0.0 copy-start.3
  1.0 0.0 copy-start.4
  1.1 14.4 %all_to_all.10.x_ref = bf16[8,3,8,512]{3,2,1,0:T(8,128)(2,1)S(1)} all-to-all(bf16[8,3,8,512]{3,2,1,0:T(8,128)(2,1)S(1)} %bitcast.9), channel_id=1, replica_groups=mesh['y_lo'=2,'z'=8,'core'=2,'y_hi'=2,'x'=4] {'y_hi','x'}, dimensions={0} | all-to-all | bytes 393216 | tf_op jit(solution)/shard_map/all_to_all | solution.py:189
  15.5 0.0 copy-done.2
  15.5 0.0 copy-done
  15.5 0.0 copy-done.1
  15.5 0.0 copy-done.3
  15.5 0.0 copy-done.4
  15.5 2.7 %first.1 = (bf16[16,8,8,128]{3,2,1,0:T(8,128)(2,1)S(1)}, f32[3,4,64,128]{3,2,1,0:T(8,128)S(1)}, bf16[3,3,4,64,128]{4,3,2,1,0:T(8,128)(2,1)S(1)}, bf16[12,128,128]{2,1,0:T(8,128)(2,1)S(1)}) custom-call(s32[8]{0:T(128)S(1)} %copy-done.1, f32[4,3]{1,0:T(4,128)S(1)} %copy-done, f32[1,512]{1,0:T(1,128)S(1)} %copy-done.4, ...), custom_call_target="tpu_custom_call" | custom-call | flops 3000000000 | bytes 2097152 | tf_op jit(solution)/shard_map/first/pallas_call | solution.py:150
  18.2 0.1 collective-permute-start
  18.3 2.2 %second.1 = f32[16,8,8,128]{3,2,1,0:T(8,128)S(1)} custom-call(f32[3,4,64,128]{3,2,1,0:T(8,128)S(1)} %get-tuple-element.9.wide, bf16[3,3,4,64,128]{4,3,2,1,0:T(8,128)(2,1)S(1)} %get-tuple-element.10.grads, bf16[12,128,128]{2,1,0:T(8,128)(2,1)S(1)} %get-tuple-element.11.tests), custom_call_target="tpu_custom_call" | custom-call | flops 2000000000 | bytes 2097152 | tf_op jit(solution)/shard_map/second/pallas_call | solution.py:168
  20.5 0.0 collective-permute-done
  20.6 0.1 add_convert_fusion
  20.6 26.8 %all_to_all.11 = bf16[128,8,128]{2,1,0:T(8,128)(2,1)S(1)} all-to-all(bf16[128,8,128]{2,1,0:T(8,128)(2,1)S(1)} %bitcast.8), channel_id=1, replica_groups=mesh['y_lo'=2,'z'=8,'core'=2,'y_hi'=2,'x'=4] {'y_lo','z','y_hi','x'}, dimensions={0} | all-to-all | bytes 524288 | tf_op jit(solution)/shard_map/all_to_all | solution.py:196
  47.4 0.1 convert_reduce_fusion
  47.6 0.7 %mul.12 = f32[8,2,64]{2,1,0:T(2,128)} reshape(f32[8,128]{1,0:T(8,128)S(1)} %broadcast_multiply_fusion) | data formatting | bytes 8192 | tf_op jit(solution)/shard_map/mul | solution.py:198
  (1 shorter events, 0.0 us)
Async XLA Ops:
  0.0 15.5 %copy-start.2 = (bf16[512,512]{1,0:T(8,128)(2,1)S(1)}, bf16[512,512]{1,0:T(8,128)(2,1)}, u32[]{:S(2)}) copy-start(bf16[512,512]{1,0:T(8,128)(2,1)} %constant.16.tt_ref) | copy-start | bytes 1572868
  1.0 14.5 %copy-start = (f32[4,3]{1,0:T(4,128)S(1)}, f32[4,3]{1,0:T(4,128)}, u32[]{:S(2)}) copy-start(f32[4,3]{1,0:T(4,128)} %types_ref.1) | copy-start | bytes 148
  1.0 14.4 %copy-start.1 = (s32[8]{0:T(128)S(1)}, s32[8]{0:T(128)}, u32[]{:S(2)}) copy-start(s32[8]{0:T(128)} %kinds_ref.1) | copy-start | bytes 100
  1.0 14.4 %copy-start.3 = (bf16[128,256]{1,0:T(8,128)(2,1)S(1)}, bf16[128,256]{1,0:T(8,128)(2,1)}, u32[]{:S(2)}) copy-start(bf16[128,256]{1,0:T(8,128)(2,1)} %constant.15.rs_ref) | copy-start | bytes 196612
  1.0 14.4 %copy-start.4 = (f32[1,512]{1,0:T(1,128)S(1)}, f32[1,512]{1,0:T(1,128)}, u32[]{:S(2)}) copy-start(f32[1,512]{1,0:T(1,128)} %constant.14.weights_ref) | copy-start | bytes 6148
  18.2 2.4 %collective-permute-start = (bf16[16,8,8,128]{3,2,1,0:T(8,128)(2,1)S(1)}, bf16[16,8,8,128]{3,2,1,0:T(8,128)(2,1)S(1)}, u32[]{:S(2)}, u32[]{:S(2)}) collective-permute-start(bf16[16,8,8,128]{3,2,1,0:T(8,128)(2,1)S(1)} %get-tuple-element.12), channel_id=1, source_target_pairs={{0,8},{8,0},{1,9},{9,1},{2,10},{10,2},{3,11},{11,3},{4,12},{12,4},... | collective-permute-start | bytes 786440 | tf_op jit(solution)/shard_map/ppermute | solution.py:193

commit v4 on v3

--- a/solution.py
+++ b/solution.py
@@ -89,8 +89,7 @@
             ],
             axis=1,
         )
-        both = lax.dot_general(left, right, (((1,), (1,)), ((), ())), preferred_element_type=f32)
-        result = both[:MODES] + both[MODES:]
+        result = lax.dot_general(left, right, (((1,), (1,)), ((), ())), preferred_element_type=f32)
         for a in range(2):
             block = result[:, a * LANES : (a + 1) * LANES]
             out_ref[2 * pair + a] = block.reshape(8, 8, LANES).astype(out_ref.dtype)
@@ -115,14 +114,11 @@
         rows = jnp.concatenate([x_ref[s, c].astype(f32) for s in range(8)], axis=0)
         turned = jnp.where(high, pltpu.roll(rows, 2, 0), pltpu.roll(rows, MODES - 2, 0))
         turned = jnp.where(swap, turned, rows)
-        weighted = rows * quad
-        upper = weighted.astype(bf16)
-        lower = (weighted - upper.astype(f32)).astype(bf16)
+        weighted = (rows * quad).astype(bf16)
         for b in range(blocks):
             at = slice(b * LANES, (b + 1) * LANES)
             wide[c, b] = turned[:, at]
-            tests[c * blocks + b, :MODES] = upper[:, at]
-            tests[c * blocks + b, MODES:] = lower[:, at]
+            tests[c * blocks + b] = weighted[:, at]
         narrow.append(rows.astype(bf16))
     panel = jnp.concatenate(narrow, axis=0)
     along_t = jnp.dot(panel, tt_ref[...], preferred_element_type=f32)
@@ -150,10 +146,10 @@
     return pl.pallas_call(
         first_kernel,
         out_shape=(
-            jax.ShapeDtypeStruct(SHAPE, jnp.bfloat16),
+            jax.ShapeDtypeStruct(SHAPE, jnp.float32),
             jax.ShapeDtypeStruct((3, blocks, MODES, LANES), jnp.float32),
             jax.ShapeDtypeStruct((3, 3, blocks, MODES, LANES), jnp.bfloat16),
-            jax.ShapeDtypeStruct((3 * blocks, 2 * MODES, LANES), jnp.bfloat16),
+            jax.ShapeDtypeStruct((3 * blocks, MODES, LANES), jnp.bfloat16),
         ),
         in_specs=[vmem] * 6,
         out_specs=(vmem,) * 4,

time: 48.4 us -> 48 us (level)
  transfers between devices with their start and end apart: 1 -> 1, of which waited for: 0 -> 0; matrix products, arithmetic and copies ran while one was open for 0% -> 0% of each run, Pallas kernels for 5% -> 4%
where the time goes in v4:
time: 48 us; the launch traced here: 47.8 us
  blocking collectives  41.2 us (86%)
  Pallas kernels  4.55 us (9%)
  local copies, waits for them, and re-layouts  1.71 us (4%)
    all_to_all x1, blocking collectives, body(): chunks = lax.all_to_all(both.reshape(128, 8, LANES), REST, 0, 0, tiled=True)  26.8 us
    all_to_all x1, blocking collectives, body(): fields = lax.all_to_all(pieces, TEST, 0, 0, tiled=True)  14.4 us
    pallas_call x1, Pallas kernels, first_half(): pl.pallas_call(first_kernel, out_shape=(jax.ShapeDtypeStruct(SHAPE, jnp.f...  2.5 us
    pallas_call x1, Pallas kernels, second_half(): pl.pallas_call(second_kernel, out_shape=jax.ShapeDtypeStruct(SHAPE, jnp.f...  2.05 us
    reshape x1, local copies, waits for them, and re-layouts, body(): pieces = mode_fields.reshape(8, 3, 8, CUBE).transpose(2, 1, 0, 3)  1 us
  transfers between devices with their start and end apart: 1, of which 0 were waited for; matrix products, arithmetic and copies ran while one was open for 0% of the time, Pallas kernels for 4%

profile of v4, /device:TPU:8, one launch (start us, length us, event | category | flops | bytes accessed | tf_op | source)
XLA Modules:
  0.0 47.8 jit_solution(15876021492522695645)
XLA Ops:
  0.0 0.0 copy-start.2
  0.0 1.0 %copy.10 = bf16[3,1,8,8,512]{4,3,1,0,2:T(8,128)(2,1)S(1)} copy(bf16[3,1,8,8,512]{4,3,2,1,0:T(8,128)(2,1)} %bitcast.10) | data formatting | bytes 393216 | tf_op jit(solution)/shard_map/reshape | solution.py:184
  1.0 0.0 copy-start
  1.0 0.0 copy-start.1
  1.0 0.0 copy-start.3
  1.0 0.0 copy-start.4
  1.1 14.4 %all_to_all.10.x_ref = bf16[8,3,8,512]{3,2,1,0:T(8,128)(2,1)S(1)} all-to-all(bf16[8,3,8,512]{3,2,1,0:T(8,128)(2,1)S(1)} %bitcast.9), channel_id=1, replica_groups=mesh['y_lo'=2,'z'=8,'core'=2,'y_hi'=2,'x'=4] {'y_hi','x'}, dimensions={0} | all-to-all | bytes 393216 | tf_op jit(solution)/shard_map/all_to_all | solution.py:185
  15.5 0.0 copy-done.2
  15.5 0.0 copy-done
  15.5 0.0 copy-done.1
  15.5 0.0 copy-done.3
  15.5 0.0 copy-done.4
  15.5 2.5 %first.1 = (f32[16,8,8,128]{3,2,1,0:T(8,128)S(1)}, f32[3,4,64,128]{3,2,1,0:T(8,128)S(1)}, bf16[3,3,4,64,128]{4,3,2,1,0:T(8,128)(2,1)S(1)}, bf16[12,64,128]{2,1,0:T(8,128)(2,1)S(1)}) custom-call(s32[8]{0:T(128)S(1)} %copy-done.1, f32[4,3]{1,0:T(4,128)S(1)} %copy-done, f32[1,512]{1,0:T(1,128)S(1)} %copy-done.4, bf16[8,3,8,512]{3,2,1,0:T(8,128)(2,1)S(1)} %all_to_all.10.x_ref, ...), custom_call_target="tpu_custom_call" | custom-call | flops 3000000000 | bytes 2097152 | tf_op jit(solution)/shard_map/first/pallas_call | solution.py:146
  18.0 0.1 collective-permute-start
  18.1 2.1 %second.1 = f32[16,8,8,128]{3,2,1,0:T(8,128)S(1)} custom-call(f32[3,4,64,128]{3,2,1,0:T(8,128)S(1)} %get-tuple-element.9.wide, bf16[3,3,4,64,128]{4,3,2,1,0:T(8,128)(2,1)S(1)} %get-tuple-element.10.grads, bf16[12,64,128]{2,1,0:T(8,128)(2,1)S(1)} %get-tuple-element.11.tests), custom_call_target="tpu_custom_call" | custom-call | flops 2000000000 | bytes 2097152 | tf_op jit(solution)/shard_map/second/pallas_call | solution.py:164
  20.1 0.0 collective-permute-done
  20.1 0.1 add_convert_fusion
  20.2 26.8 %all_to_all.11 = bf16[128,8,128]{2,1,0:T(8,128)(2,1)S(1)} all-to-all(bf16[128,8,128]{2,1,0:T(8,128)(2,1)S(1)} %bitcast.8), channel_id=1, replica_groups=mesh['y_lo'=2,'z'=8,'core'=2,'y_hi'=2,'x'=4] {'y_lo','z','y_hi','x'}, dimensions={0} | all-to-all | bytes 524288 | tf_op jit(solution)/shard_map/all_to_all | solution.py:192
  47.0 0.1 convert_reduce_fusion
  47.1 0.7 %mul.12 = f32[8,2,64]{2,1,0:T(2,128)} reshape(f32[8,128]{1,0:T(8,128)S(1)} %broadcast_multiply_fusion) | data formatting | bytes 8192 | tf_op jit(solution)/shard_map/mul | solution.py:194
  (1 shorter events, 0.0 us)
Async XLA Ops:
  0.0 15.5 %copy-start.2 = (bf16[512,512]{1,0:T(8,128)(2,1)S(1)}, bf16[512,512]{1,0:T(8,128)(2,1)}, u32[]{:S(2)}) copy-start(bf16[512,512]{1,0:T(8,128)(2,1)} %constant.16.tt_ref) | copy-start | bytes 1572868
  1.0 14.5 %copy-start = (f32[4,3]{1,0:T(4,128)S(1)}, f32[4,3]{1,0:T(4,128)}, u32[]{:S(2)}) copy-start(f32[4,3]{1,0:T(4,128)} %types_ref.1) | copy-start | bytes 148
  1.0 14.4 %copy-start.1 = (s32[8]{0:T(128)S(1)}, s32[8]{0:T(128)}, u32[]{:S(2)}) copy-start(s32[8]{0:T(128)} %kinds_ref.1) | copy-start | bytes 100
  1.0 14.4 %copy-start.3 = (bf16[128,256]{1,0:T(8,128)(2,1)S(1)}, bf16[128,256]{1,0:T(8,128)(2,1)}, u32[]{:S(2)}) copy-start(bf16[128,256]{1,0:T(8,128)(2,1)} %constant.15.rs_ref) | copy-start | bytes 196612
  1.0 14.4 %copy-start.4 = (f32[1,512]{1,0:T(1,128)S(1)}, f32[1,512]{1,0:T(1,128)}, u32[]{:S(2)}) copy-start(f32[1,512]{1,0:T(1,128)} %constant.14.weights_ref) | copy-start | bytes 6148
  18.0 2.2 %collective-permute-start = (f32[16,8,8,128]{3,2,1,0:T(8,128)S(1)}, f32[16,8,8,128]{3,2,1,0:T(8,128)S(1)}, u32[]{:S(2)}, u32[]{:S(2)}) collective-permute-start(f32[16,8,8,128]{3,2,1,0:T(8,128)S(1)} %get-tuple-element.12), channel_id=1, source_target_pairs={{0,8},{8,0},{1,9},{9,1},{2,10},{10,2},{3,11},{11,3},{4,12},{12,4},... | collective-permute-start | bytes 1572872 | tf_op jit(solution)/shard_map/ppermute | solution.py:189

commit v5 on v4

--- a/solution.py
+++ b/solution.py
@@ -172,6 +172,29 @@
     )(wide, grads, tests)
 
 
+def total_kernel(norm, chunks_ref, out_ref):
+    sums = [jnp.zeros((8, LANES), jnp.float32) for _ in range(8)]
+    for n in range(8 * OWNERS):
+        sums[n % 8] = sums[n % 8] + chunks_ref[n].astype(jnp.float32)
+    while len(sums) > 1:
+        sums = [sums[n] + sums[n + 1] for n in range(0, len(sums), 2)]
+    result = sums[0] * norm
+    for jj in range(2):
+        out_ref[:, jj, :] = result[:, jj * MODES : (jj + 1) * MODES]
+
+
+def totalled(chunks, norm):
+    vmem = pl.BlockSpec(memory_space=pltpu.VMEM)
+    return pl.pallas_call(
+        functools.partial(total_kernel, norm),
+        out_shape=jax.ShapeDtypeStruct((8, 2, MODES), jnp.float32),
+        in_specs=[vmem],
+        out_specs=vmem,
+        compiler_params=pltpu.CompilerParams(vmem_limit_bytes=8 * 2**20),
+        name="total",
+    )(chunks)
+
+
 REST = ("y_lo", "z", "y_hi", "x")
 
 
@@ -190,8 +213,7 @@
     own = second_half(wide, grads, tests)
     both = (own + other.astype(jnp.float32)).astype(bf16)
     chunks = lax.all_to_all(both.reshape(128, 8, LANES), REST, 0, 0, tiled=True)
-    summed = jnp.sum(chunks.astype(jnp.float32), axis=0)
-    return (summed * float(total_points) ** (-0.5)).reshape(8, 2, MODES)
+    return totalled(chunks, float(total_points) ** (-0.5))
 
 
 def solution(mesh):

time: 48 us -> 47.9 us (level)
  Pallas kernels: 4.55 us -> 5.27 us
  local copies, waits for them, and re-layouts: 1.71 us -> 1.03 us
    pallas_call x0 -> x1, Pallas kernels: none -> 0.71 us  [totalled(): pl.pallas_call(functools.partial(total_kernel, norm), out_shape=jax.Shape...]
    mul x1 -> x0, local copies, waits for them, and re-layouts: 0.68 us -> none  [body(): return (summed * float(total_points) ** (-0.5)).reshape(8, 2, MODES)]
where the time goes in v5:
time: 47.9 us; the launch traced here: 47.7 us
  blocking collectives  41.2 us (86%)
  Pallas kernels  5.27 us (11%)
  local copies, waits for them, and re-layouts  1.03 us (2%)
    all_to_all x1, blocking collectives, body(): chunks = lax.all_to_all(both.reshape(128, 8, LANES), REST, 0, 0, tiled=True)  26.8 us
    all_to_all x1, blocking collectives, body(): fields = lax.all_to_all(pieces, TEST, 0, 0, tiled=True)  14.4 us
    pallas_call x1, Pallas kernels, first_half(): pl.pallas_call(first_kernel, out_shape=(jax.ShapeDtypeStruct(SHAPE, jnp.f...  2.5 us
    pallas_call x1, Pallas kernels, second_half(): pl.pallas_call(second_kernel, out_shape=jax.ShapeDtypeStruct(SHAPE, jnp.f...  2.05 us
    reshape x1, local copies, waits for them, and re-layouts, body(): pieces = mode_fields.reshape(8, 3, 8, CUBE).transpose(2, 1, 0, 3)  1 us
  transfers between devices with their start and end apart: 1, of which 0 were waited for; matrix products, arithmetic and copies ran while one was open for 0% of the time, Pallas kernels for 4%

profile of v5, /device:TPU:8, one launch (start us, length us, event | category | flops | bytes accessed | tf_op | source)
XLA Modules:
  0.0 47.7 jit_solution(10525617515078200939)
XLA Ops:
  0.0 0.0 copy-start.2
  0.0 1.0 %copy.10 = bf16[3,1,8,8,512]{4,3,1,0,2:T(8,128)(2,1)S(1)} copy(bf16[3,1,8,8,512]{4,3,2,1,0:T(8,128)(2,1)} %bitcast.10) | data formatting | bytes 393216 | tf_op jit(solution)/shard_map/reshape | solution.py:207
  1.0 0.0 copy-start
  1.0 0.0 copy-start.1
  1.0 0.0 copy-start.3
  1.0 0.0 copy-start.4
  1.1 14.4 %all_to_all.10.x_ref = bf16[8,3,8,512]{3,2,1,0:T(8,128)(2,1)S(1)} all-to-all(bf16[8,3,8,512]{3,2,1,0:T(8,128)(2,1)S(1)} %bitcast.9), channel_id=1, replica_groups=mesh['y_lo'=2,'z'=8,'core'=2,'y_hi'=2,'x'=4] {'y_hi','x'}, dimensions={0} | all-to-all | bytes 393216 | tf_op jit(solution)/shard_map/all_to_all | solution.py:208
  15.5 0.0 copy-done.2
  15.5 0.0 copy-done
  15.5 0.0 copy-done.1
  15.5 0.0 copy-done.3
  15.5 0.0 copy-done.4
  15.5 2.5 %first.1 = (f32[16,8,8,128]{3,2,1,0:T(8,128)S(1)}, f32[3,4,64,128]{3,2,1,0:T(8,128)S(1)}, bf16[3,3,4,64,128]{4,3,2,1,0:T(8,128)(2,1)S(1)}, bf16[12,64,128]{2,1,0:T(8,128)(2,1)S(1)}) custom-call(s32[8]{0:T(128)S(1)} %copy-done.1, f32[4,3]{1,0:T(4,128)S(1)} %copy-done, f32[1,512]{1,0:T(1,128)S(1)} %copy-done.4, bf16[8,3,8,512]{3,2,1,0:T(8,128)(2,1)S(1)} %all_to_all.10.x_ref, ...), custom_call_target="tpu_custom_call" | custom-call | flops 3000000000 | bytes 2097152 | tf_op jit(solution)/shard_map/first/pallas_call | solution.py:146
  18.0 0.1 collective-permute-start
  18.1 2.1 %second.1 = f32[16,8,8,128]{3,2,1,0:T(8,128)S(1)} custom-call(f32[3,4,64,128]{3,2,1,0:T(8,128)S(1)} %get-tuple-element.9.wide, bf16[3,3,4,64,128]{4,3,2,1,0:T(8,128)(2,1)S(1)} %get-tuple-element.10.grads, bf16[12,64,128]{2,1,0:T(8,128)(2,1)S(1)} %get-tuple-element.11.tests), custom_call_target="tpu_custom_call" | custom-call | flops 2000000000 | bytes 2097152 | tf_op jit(solution)/shard_map/second/pallas_call | solution.py:164
  20.1 0.0 collective-permute-done
  20.1 0.1 add_convert_fusion
  20.2 26.8 %all_to_all.11.chunks_ref = bf16[128,8,128]{2,1,0:T(8,128)(2,1)S(1)} all-to-all(bf16[128,8,128]{2,1,0:T(8,128)(2,1)S(1)} %bitcast.8), channel_id=1, replica_groups=mesh['y_lo'=2,'z'=8,'core'=2,'y_hi'=2,'x'=4] {'y_lo','z','y_hi','x'}, dimensions={0} | all-to-all | bytes 524288 | tf_op jit(solution)/shard_map/all_to_all | solution.py:215
  47.0 0.7 %total.1 = f32[8,2,64]{2,1,0:T(2,128)} custom-call(bf16[128,8,128]{2,1,0:T(8,128)(2,1)S(1)} %all_to_all.11.chunks_ref), custom_call_target="tpu_custom_call" | custom-call | tf_op jit(solution)/shard_map/total/pallas_call | solution.py:188
Async XLA Ops:
  0.0 15.5 %copy-start.2 = (bf16[512,512]{1,0:T(8,128)(2,1)S(1)}, bf16[512,512]{1,0:T(8,128)(2,1)}, u32[]{:S(2)}) copy-start(bf16[512,512]{1,0:T(8,128)(2,1)} %constant.12.tt_ref) | copy-start | bytes 1572868
  1.0 14.5 %copy-start = (f32[4,3]{1,0:T(4,128)S(1)}, f32[4,3]{1,0:T(4,128)}, u32[]{:S(2)}) copy-start(f32[4,3]{1,0:T(4,128)} %types_ref.1) | copy-start | bytes 148
  1.0 14.4 %copy-start.1 = (s32[8]{0:T(128)S(1)}, s32[8]{0:T(128)}, u32[]{:S(2)}) copy-start(s32[8]{0:T(128)} %kinds_ref.1) | copy-start | bytes 100
  1.0 14.4 %copy-start.3 = (bf16[128,256]{1,0:T(8,128)(2,1)S(1)}, bf16[128,256]{1,0:T(8,128)(2,1)}, u32[]{:S(2)}) copy-start(bf16[128,256]{1,0:T(8,128)(2,1)} %constant.11.rs_ref) | copy-start | bytes 196612
  1.0 14.4 %copy-start.4 = (f32[1,512]{1,0:T(1,128)S(1)}, f32[1,512]{1,0:T(1,128)}, u32[]{:S(2)}) copy-start(f32[1,512]{1,0:T(1,128)} %constant.10.weights_ref) | copy-start | bytes 6148
  18.0 2.2 %collective-permute-start = (f32[16,8,8,128]{3,2,1,0:T(8,128)S(1)}, f32[16,8,8,128]{3,2,1,0:T(8,128)S(1)}, u32[]{:S(2)}, u32[]{:S(2)}) collective-permute-start(f32[16,8,8,128]{3,2,1,0:T(8,128)S(1)} %get-tuple-element.12), channel_id=1, source_target_pairs={{0,8},{8,0},{1,9},{9,1},{2,10},{10,2},{3,11},{11,3},{4,12},{12,4},... | collective-permute-start | bytes 1572872 | tf_op jit(solution)/shard_map/ppermute | solution.py:212

commit v6 on v5

--- a/solution.py
+++ b/solution.py
@@ -146,7 +146,7 @@
     return pl.pallas_call(
         first_kernel,
         out_shape=(
-            jax.ShapeDtypeStruct(SHAPE, jnp.float32),
+            jax.ShapeDtypeStruct(SHAPE, jnp.bfloat16),
             jax.ShapeDtypeStruct((3, blocks, MODES, LANES), jnp.float32),
             jax.ShapeDtypeStruct((3, 3, blocks, MODES, LANES), jnp.bfloat16),
             jax.ShapeDtypeStruct((3 * blocks, MODES, LANES), jnp.bfloat16),

time: 47.9 us -> 47.9 us (level)
  no operation moved by 1% of the time
where the time goes in v6:
time: 47.9 us; the launch traced here: 47.7 us
  blocking collectives  41.2 us (86%)
  Pallas kernels  5.27 us (11%)
  local copies, waits for them, and re-layouts  1.03 us (2%)
    all_to_all x1, blocking collectives, body(): chunks = lax.all_to_all(both.reshape(128, 8, LANES), REST, 0, 0, tiled=True)  26.8 us
    all_to_all x1, blocking collectives, body(): fields = lax.all_to_all(pieces, TEST, 0, 0, tiled=True)  14.4 us
    pallas_call x1, Pallas kernels, first_half(): pl.pallas_call(first_kernel, out_shape=(jax.ShapeDtypeStruct(SHAPE, jnp.b...  2.51 us
    pallas_call x1, Pallas kernels, second_half(): pl.pallas_call(second_kernel, out_shape=jax.ShapeDtypeStruct(SHAPE, jnp.f...  2.05 us
    reshape x1, local copies, waits for them, and re-layouts, body(): pieces = mode_fields.reshape(8, 3, 8, CUBE).transpose(2, 1, 0, 3)  1 us
  transfers between devices with their start and end apart: 1, of which 0 were waited for; matrix products, arithmetic and copies ran while one was open for 0% of the time, Pallas kernels for 4%

profile of v6, /device:TPU:8, one launch (start us, length us, event | category | flops | bytes accessed | tf_op | source)
XLA Modules:
  0.0 47.7 jit_solution(13284153099748573941)
XLA Ops:
  0.0 0.0 copy-start.2
  0.0 1.0 %copy.10 = bf16[3,1,8,8,512]{4,3,1,0,2:T(8,128)(2,1)S(1)} copy(bf16[3,1,8,8,512]{4,3,2,1,0:T(8,128)(2,1)} %bitcast.10) | data formatting | bytes 393216 | tf_op jit(solution)/shard_map/reshape | solution.py:207
  1.0 0.0 copy-start
  1.0 0.0 copy-start.1
  1.0 0.0 copy-start.3
  1.0 0.0 copy-start.4
  1.1 14.4 %all_to_all.10.x_ref = bf16[8,3,8,512]{3,2,1,0:T(8,128)(2,1)S(1)} all-to-all(bf16[8,3,8,512]{3,2,1,0:T(8,128)(2,1)S(1)} %bitcast.9), channel_id=1, replica_groups=mesh['y_lo'=2,'z'=8,'core'=2,'y_hi'=2,'x'=4] {'y_hi','x'}, dimensions={0} | all-to-all | bytes 393216 | tf_op jit(solution)/shard_map/all_to_all | solution.py:208
  15.5 0.0 copy-done.2
  15.5 0.0 copy-done
  15.5 0.0 copy-done.1
  15.5 0.0 copy-done.3
  15.5 0.0 copy-done.4
  15.5 2.5 %first.1 = (bf16[16,8,8,128]{3,2,1,0:T(8,128)(2,1)S(1)}, f32[3,4,64,128]{3,2,1,0:T(8,128)S(1)}, bf16[3,3,4,64,128]{4,3,2,1,0:T(8,128)(2,1)S(1)}, bf16[12,64,128]{2,1,0:T(8,128)(2,1)S(1)}) custom-call(s32[8]{0:T(128)S(1)} %copy-done.1, f32[4,3]{1,0:T(4,128)S(1)} %copy-done, f32[1,512]{1,0:T(1,128)S(1)} %copy-done.4, ...), custom_call_target="tpu_custom_call" | custom-call | flops 3000000000 | bytes 2097152 | tf_op jit(solution)/shard_map/first/pallas_call | solution.py:146
  18.0 0.1 collective-permute-start
  18.1 2.0 %second.1 = f32[16,8,8,128]{3,2,1,0:T(8,128)S(1)} custom-call(f32[3,4,64,128]{3,2,1,0:T(8,128)S(1)} %get-tuple-element.9.wide, bf16[3,3,4,64,128]{4,3,2,1,0:T(8,128)(2,1)S(1)} %get-tuple-element.10.grads, bf16[12,64,128]{2,1,0:T(8,128)(2,1)S(1)} %get-tuple-element.11.tests), custom_call_target="tpu_custom_call" | custom-call | flops 2000000000 | bytes 2097152 | tf_op jit(solution)/shard_map/second/pallas_call | solution.py:164
  20.1 0.0 collective-permute-done
  20.2 0.1 add_convert_fusion
  20.2 26.8 %all_to_all.11.chunks_ref = bf16[128,8,128]{2,1,0:T(8,128)(2,1)S(1)} all-to-all(bf16[128,8,128]{2,1,0:T(8,128)(2,1)S(1)} %bitcast.8), channel_id=1, replica_groups=mesh['y_lo'=2,'z'=8,'core'=2,'y_hi'=2,'x'=4] {'y_lo','z','y_hi','x'}, dimensions={0} | all-to-all | bytes 524288 | tf_op jit(solution)/shard_map/all_to_all | solution.py:215
  47.0 0.7 %total.1 = f32[8,2,64]{2,1,0:T(2,128)} custom-call(bf16[128,8,128]{2,1,0:T(8,128)(2,1)S(1)} %all_to_all.11.chunks_ref), custom_call_target="tpu_custom_call" | custom-call | tf_op jit(solution)/shard_map/total/pallas_call | solution.py:188
Async XLA Ops:
  0.0 15.5 %copy-start.2 = (bf16[512,512]{1,0:T(8,128)(2,1)S(1)}, bf16[512,512]{1,0:T(8,128)(2,1)}, u32[]{:S(2)}) copy-start(bf16[512,512]{1,0:T(8,128)(2,1)} %constant.12.tt_ref) | copy-start | bytes 1572868
  1.0 14.5 %copy-start = (f32[4,3]{1,0:T(4,128)S(1)}, f32[4,3]{1,0:T(4,128)}, u32[]{:S(2)}) copy-start(f32[4,3]{1,0:T(4,128)} %types_ref.1) | copy-start | bytes 148
  1.0 14.4 %copy-start.1 = (s32[8]{0:T(128)S(1)}, s32[8]{0:T(128)}, u32[]{:S(2)}) copy-start(s32[8]{0:T(128)} %kinds_ref.1) | copy-start | bytes 100
  1.0 14.4 %copy-start.3 = (bf16[128,256]{1,0:T(8,128)(2,1)S(1)}, bf16[128,256]{1,0:T(8,128)(2,1)}, u32[]{:S(2)}) copy-start(bf16[128,256]{1,0:T(8,128)(2,1)} %constant.11.rs_ref) | copy-start | bytes 196612
  1.0 14.4 %copy-start.4 = (f32[1,512]{1,0:T(1,128)S(1)}, f32[1,512]{1,0:T(1,128)}, u32[]{:S(2)}) copy-start(f32[1,512]{1,0:T(1,128)} %constant.10.weights_ref) | copy-start | bytes 6148
  18.0 2.2 %collective-permute-start = (bf16[16,8,8,128]{3,2,1,0:T(8,128)(2,1)S(1)}, bf16[16,8,8,128]{3,2,1,0:T(8,128)(2,1)S(1)}, u32[]{:S(2)}, u32[]{:S(2)}) collective-permute-start(bf16[16,8,8,128]{3,2,1,0:T(8,128)(2,1)S(1)} %get-tuple-element.12), channel_id=1, source_target_pairs={{0,8},{8,0},{1,9},{9,1},{2,10},{10,2},{3,11},{11,3},{4,12},{12,4},... | collective-permute-start | bytes 786440 | tf_op jit(solution)/shard_map/ppermute | solution.py:212
